TPU v7x, 512 devices: a whole 4x4x16 slice. The times are simulated.
512 devices in a mesh: seq: 128 (over z_lo, y, x), tp: 4 (over z_hi, core).
Axes of the slice: x: 4, y: 4, z: 16 (z_hi: 2, z_lo: 8; z = z_hi * 8 + z_lo), core: 2. Of those that a mesh axis runs over, the one named last changes fastest.
Arguments:
- inputs: bfloat16 [32768, 5120], P('seq', 'tp'), may hold values from -6 to 6
- gate_input: bfloat16 [32768, 5120], P('seq', 'tp'), may hold values from -6 to 6
- b_source: bfloat16 [32768, 128], P('seq'), may hold values from -6 to 6
- c_source: bfloat16 [32768, 128], P('seq'), may hold values from -6 to 6
- step_raw: float32 [32768, 80], P('seq', 'tp'), may hold values from -4 to 4
- step_bias: float32 [80], P('tp'), may hold values from -3 to 0
- decay_rate: float32 [80], P('tp'), may hold values from 6.1035157e-06 to 0.05
- conv_weight: float32 [4, 256], replicated, may hold values from -3 to 3
- conv_bias: float32 [256], replicated, may hold values from -3 to 3
- norm_gain: float32 [5120], P('tp'), may hold values from 0.5 to 1.5
- doc_lengths: int32 [8], replicated, may hold values from 1 to 16384, 32768 in all
Outputs:
- output: bfloat16 [32768, 5120], P('seq', 'tp')
Inputs may be any that keep to these rules, and one draw needn't show every extreme that they name: doc_lengths sums to 32768; every length is at least 1 and the largest is exactly 16384.
All inputs are finite; a program needn't handle non-finite values.
Results may differ from a plain program's by a relative error of at most 0.0015.
Values may be sent and summed in bfloat16 or wider, within the bound.
A program may use at most 192 MiB of HBM per device.

v0:
```python
import jax
import jax.numpy as jnp
from jax import lax
from jax.sharding import Mesh
from jax.sharding import PartitionSpec as P

BLOCK = 256
SEQ = ("seq_0", "seq_1", "seq_2")


epsilon = 1e-05


def nothing_yet(array, identity):
    return jax.tree.map(
        lambda a, e: jnp.broadcast_to(jnp.asarray(e, a.dtype), a.shape), array, identity
    )


def carried_in(array, axes, combine, identity, reverse):
    before = start = nothing_yet(array, identity)
    so_far = array
    for axis in reversed(axes):
        size, place = lax.axis_size(axis), lax.axis_index(axis)
        pieces = jax.tree.map(lambda part: lax.all_gather(part, axis), so_far)
        inside, so_far = start, start
        for k in reversed(range(size)) if reverse else range(size):
            passed = k > place if reverse else k < place
            so_far = combine(so_far, jax.tree.map(lambda part: part[k], pieces))
            inside = jax.tree.map(lambda new, old: jnp.where(passed, new, old), so_far, inside)
        before = combine(inside, before)
    return before


def from_behind(value, axis, steps):
    count = lax.axis_size(axis)
    first, last = max(0, -steps), min(count, count - steps)
    return lax.ppermute(value, axis, [(source, source + steps) for source in range(first, last)])


def gathered_total(array, axis):
    parts = lax.all_gather(array, axis)
    return parts.sum(axis=0)


def locate(position, doc_lengths):
    starts = (jnp.cumsum(doc_lengths) - doc_lengths).astype(jnp.int32)
    chosen = jnp.where(starts[None, :] <= position[:, None], starts[None, :], 0)
    return jnp.max(chosen, axis=1).astype(jnp.int32)


def convolve(padded, weight, conv_bias, position, doc_start):
    kernel_taps = weight.shape[0]
    tokens = position.shape[0]
    widened = padded.astype(jnp.float32)
    summed = jnp.broadcast_to(conv_bias[None, :], (tokens, conv_bias.shape[0]))
    for offset in range(kernel_taps):
        backward = kernel_taps - 1 - offset
        inside = (position - backward >= doc_start)[:, None]
        summed = summed + jnp.where(
            inside, weight[offset][None, :] * widened[offset : offset + tokens], 0.0
        )
    return jax.nn.silu(summed).astype(jnp.bfloat16)


def state_terms(pieces):
    block_inputs, b_block, step_size, cumulated, doc_start, position = pieces
    same_doc = doc_start == doc_start[-1]
    weighting = jnp.where(
        same_doc[:, None], jnp.exp(cumulated[-1][None, :] - cumulated) * step_size, 0.0
    )
    weighted = (block_inputs.astype(jnp.float32) * weighting[:, :, None]).astype(jnp.bfloat16)
    end_state = jnp.einsum("qhp,qn->hpn", weighted, b_block, preferred_element_type=jnp.float32)
    end_factor = jnp.where(doc_start[-1] < position[0], jnp.exp(cumulated[-1]), 0.0)
    return (end_state, end_factor)


def diagonal_terms(pieces):
    block_inputs, b_block, c_block, step_size, cumulated, doc_start = pieces
    row_count = doc_start.shape[0]
    products = jnp.dot(c_block, b_block.T, preferred_element_type=jnp.float32)
    order_ids = jnp.arange(row_count)
    causal = (order_ids[None, :] <= order_ids[:, None]) & (doc_start[None, :] == doc_start[:, None])
    decay_gap = cumulated.T[:, :, None] - cumulated.T[:, None, :]
    scores = jnp.where(
        causal[None], products[None] * jnp.exp(decay_gap) * step_size.T[:, None, :], 0.0
    )
    return jnp.einsum(
        "hts,shp->thp",
        scores.astype(jnp.bfloat16),
        block_inputs,
        preferred_element_type=jnp.float32,
    )


def emit_rows(state_in, pieces):
    end_state, end_factor, c_block, out_decay = pieces
    from_state = jnp.einsum(
        "qn,hpn->qhp", c_block, state_in.astype(jnp.bfloat16), preferred_element_type=jnp.float32
    )
    from_state = from_state * out_decay[:, :, None]
    return (end_factor[:, None, None] * state_in + end_state, from_state)


def fold_local(carry_pair, pieces):
    factor, state_part = carry_pair
    end_state, end_factor = pieces
    return ((factor * end_factor, end_factor[:, None, None] * state_part + end_state), None)


def combine(earlier, later):
    return (earlier[0] * later[0], later[0][:, None, None] * earlier[1] + later[1])


def carried_state(device_factor, device_state):
    identity = (jnp.ones_like(device_factor), jnp.zeros_like(device_state))
    factor_in, state_in = carried_in((device_factor, device_state), SEQ, combine, identity, False)
    return state_in


def body(
    inputs,
    gate_input,
    b_source,
    c_source,
    step_raw,
    step_bias,
    decay_rate,
    conv_weight,
    conv_bias,
    norm_gain,
    doc_lengths,
):
    tokens = inputs.shape[0]
    head_count = step_raw.shape[1]
    head_width = inputs.shape[1] // head_count
    state_width = b_source.shape[1]
    keep_rows = conv_weight.shape[0] - 1
    block_count = tokens // BLOCK
    position = lax.axis_index(SEQ) * tokens + jnp.arange(tokens, dtype=jnp.int32)
    doc_start = locate(position, doc_lengths)
    b_before = from_behind(b_source[tokens - keep_rows :], SEQ, 1)
    c_before = from_behind(c_source[tokens - keep_rows :], SEQ, 1)
    b_conv = convolve(
        jnp.concatenate([b_before, b_source], 0),
        conv_weight[:, :state_width],
        conv_bias[:state_width],
        position,
        doc_start,
    )
    c_conv = convolve(
        jnp.concatenate([c_before, c_source], 0),
        conv_weight[:, state_width:],
        conv_bias[state_width:],
        position,
        doc_start,
    )
    step_size = jax.nn.softplus(step_raw + step_bias[None, :])
    log_decay = -step_size * decay_rate[None, :]
    shaped_inputs = inputs.reshape(block_count, BLOCK, head_count, head_width)
    b_blocks = b_conv.reshape(block_count, BLOCK, state_width)
    c_blocks = c_conv.reshape(block_count, BLOCK, state_width)
    step_blocks = step_size.reshape(block_count, BLOCK, head_count)
    cumulated = jnp.cumsum(log_decay.reshape(block_count, BLOCK, head_count), axis=1)
    start_blocks = doc_start.reshape(block_count, BLOCK)
    position_blocks = position.reshape(block_count, BLOCK)
    out_decay = jnp.where(
        (start_blocks < position_blocks[:, :1])[:, :, None], jnp.exp(cumulated), 0.0
    )
    end_states, end_factors = lax.map(
        state_terms,
        (shaped_inputs, b_blocks, step_blocks, cumulated, start_blocks, position_blocks),
    )
    start_pair = (
        jnp.ones((head_count,), jnp.float32),
        jnp.zeros((head_count, head_width, state_width), jnp.float32),
    )
    device_pair, unused = lax.scan(fold_local, start_pair, (end_states, end_factors))
    diag_pieces = (shaped_inputs, b_blocks, c_blocks, step_blocks, cumulated, start_blocks)
    state_in = carried_state(device_pair[0], device_pair[1])
    diagonal = lax.map(diagonal_terms, diag_pieces)
    final_state, from_state = lax.scan(
        emit_rows, state_in, (end_states, end_factors, c_blocks, out_decay)
    )
    mixed = (diagonal + from_state).reshape(tokens, head_count * head_width)
    gated = mixed * jax.nn.silu(gate_input.astype(jnp.float32))
    square_sums = gathered_total(jnp.sum(gated * gated, axis=1), "tp")
    mean_square = square_sums / (head_count * head_width * lax.axis_size("tp"))
    return (gated * lax.rsqrt(mean_square + epsilon)[:, None] * norm_gain[None, :]).astype(
        jnp.bfloat16
    )


def solution(mesh):
    finer = Mesh(mesh.devices.reshape(8, 4, 4, mesh.shape["tp"]), ("seq_0", "seq_1", "seq_2", "tp"))
    in_specs = (
        P(SEQ, "tp"),
        P(SEQ, "tp"),
        P(SEQ, None),
        P(SEQ, None),
        P(SEQ, "tp"),
        P("tp"),
        P("tp"),
        P(),
        P(),
        P("tp"),
        P(),
    )
    out_specs = P(SEQ, "tp")
    return jax.shard_map(body, mesh=finer, in_specs=in_specs, out_specs=out_specs, check_vma=False)
```

profile of v0, /device:TPU:1, one launch (start us, length us, event | category | flops | bytes accessed | tf_op | source)
XLA Modules:
  0.0 272.8 jit_solution(13329174135072824862)
XLA Ops:
  6.5 0.8 slice.203
  7.3 3.9 %collective-permute-start.1 = (bf16[3,128]{1,0:T(4,128)(2,1)S(1)}, bf16[3,128]{1,0:T(4,128)(2,1)S(1)}, u32[]{:S(2)}, u32[]{:S(2)}) collective-permute-start(bf16[3,128]{1,0:T(4,128)(2,1)S(1)} %slice.203), channel_id=1, source_target_pairs={{0,4},{4,8},{8,12},{12,16},{16,20},{20,24},{24,28},{28,32},{32,36}... | collective-permute-start | bytes 2312 | tf_op jit(solution)/shard_map/ppermute | solution.py:38
  11.2 0.8 multiply_bitcast_fusion
  12.9 0.8 reduce-window.19
  15.8 0.7 broadcast_compare_fusion.1
  17.7 0.9 slice_bitcast_fusion.19
  18.6 0.8 fusion.62
  19.8 0.9 fusion.55
  20.7 1.3 copy.35
  22.3 1.2 convolution_add_fusion
  23.6 7.7 %all-gather = f32[4,1,20]{2,1,0:T(1,128)S(1)} all-gather(f32[1,1,20]{2,1,0:T(1,128)S(1)} %copy.36), channel_id=2, replica_groups=mesh['seq_0'=8,'seq_1'=4,'seq_2'=4,'tp'=4] {'seq_2'}, dimensions={0}, use_global_device_ids=true | all-gather | bytes 400 | tf_op jit(solution)/shard_map/all_gather | solution.py:25
  31.4 8.0 %all-gather.3 = f32[4,1,20]{2,1,0:T(1,128)S(1)} all-gather(f32[1,1,20]{2,1,0:T(1,128)S(1)} %get-tuple-element.122), channel_id=1, replica_groups=mesh['seq_0'=8,'seq_1'=4,'seq_2'=4,'tp'=4] {'seq_1'}, dimensions={0}, use_global_device_ids=true | all-gather | bytes 400 | tf_op jit(solution)/shard_map/all_gather | solution.py:25
  39.3 31.2 %all-gather.14.cloned.1.call-done = f32[80,64,128]{2,1,0:T(8,128)} async-done(((f32[20,64,128]{2,1,0:T(8,128)}), f32[80,64,128]{2,1,0:T(8,128)}) %all-gather.14.cloned.1.call-update) | async-done | bytes 2621456 | tf_op jit(solution)/shard_map/all_gather | solution.py:25
  70.5 2.8 %bitcast_add_fusion.4 = f32[1,20,64,128]{3,2,1,0:T(8,128)} fusion(f32[80,64,128]{2,1,0:T(8,128)} %all-gather.14.cloned.1.call-done, f32[20]{0:T(128)S(1)} %get-tuple-element.120, f32[20]{0:T(128)S(1)} %get-tuple-element.125, f32[20]{0:T(128)S(1)} %get-tuple-element.124, f32[20]{0:T(128)S(1)} %get-tuple-element.123), kind=kLoop, calls=%fused_computation.48 | loop fusion | flops 1146880 | bytes 3277120 | tf_op jit(solution)/shard_map/add | solution.py:112
  73.4 43.0 %all-gather.10.cloned.1.call-done = f32[4,20,64,128]{3,2,1,0:T(8,128)} async-done(((f32[1,20,64,128]{3,2,1,0:T(8,128)}), f32[4,20,64,128]{3,2,1,0:T(8,128)}) %all-gather.10.cloned.1.call-update) | async-done | bytes 2621456 | tf_op jit(solution)/shard_map/all_gather | solution.py:25
  116.4 2.8 %multiply_add_fusion = f32[1,20,64,128]{3,2,1,0:T(8,128)} fusion(f32[4,20,64,128]{3,2,1,0:T(8,128)} %all-gather.10.cloned.1.call-done, f32[20]{0:T(128)S(1)} %get-tuple-element.121, f32[20]{0:T(128)S(1)} %get-tuple-element.118, f32[20]{0:T(128)S(1)} %get-tuple-element.116, f32[20]{0:T(128)S(1)} %get-tuple-element.108), kind=kLoop, calls=%fused_computation.55 | loop fusion | flops 1146880 | bytes 3277120 | tf_op jit(solution)/shard_map/add | solution.py:112
  119.2 3.1 %collective-permute-start = (bf16[3,128]{1,0:T(4,128)(2,1)S(1)}, bf16[3,128]{1,0:T(4,128)(2,1)S(1)}, u32[]{:S(2)}, u32[]{:S(2)}) collective-permute-start(bf16[3,128]{1,0:T(4,128)(2,1)S(1)} %slice.193), channel_id=1, source_target_pairs={{0,4},{4,8},{8,12},{12,16},{16,20},{20,24},{24,28},{28,32},{32,36}... | collective-permute-start | bytes 2312 | tf_op jit(solution)/shard_map/ppermute | solution.py:38
  122.3 29.6 %all-gather.4 = f32[8,1,20]{2,1,0:T(1,128)S(1)} all-gather(f32[1,1,20]{2,1,0:T(1,128)S(1)} %get-tuple-element.107), channel_id=1, replica_groups=mesh['seq_0'=8,'seq_1'=4,'seq_2'=4,'tp'=4] {'seq_0'}, dimensions={0}, use_global_device_ids=true | all-gather | bytes 720 | tf_op jit(solution)/shard_map/all_gather | solution.py:25
  152.8 2.5 fusion.7
  155.4 85.7 %all-gather.12.cloned.1.call-done = f32[8,20,64,128]{3,2,1,0:T(8,128)} async-done(((f32[1,20,64,128]{3,2,1,0:T(8,128)}), f32[8,20,64,128]{3,2,1,0:T(8,128)}) %all-gather.12.cloned.1.call-update) | async-done | bytes 5242896 | tf_op jit(solution)/shard_map/all_gather | solution.py:25
  241.0 5.9 %fusion.8 = f32[256,20,64]{0,2,1:T(8,128)S(1)} fusion(f32[256,20,64]{0,2,1:T(8,128)} %fusion.7, f32[256,20]{0,1:T(8,128)S(1)} %get-tuple-element.135, f32[8,20,64,128]{3,2,1,0:T(8,128)} %all-gather.12.cloned.1.call-done, f32[4,20,64,128]{3,2,1,0:T(8,128)} %all-gather.10.cloned.1.call-done, f32[80,64,128]{2,1,0:T(8,128)} %all-gather.14.cloned.1.call-done, ...), kind=kOutput, calls=%fused_computation.12 | convolution fusion | flops 92733440 | bytes 13194672 | tf_op jit(solution)/shard_map/while/body/eval_jaxpr/qn,hpn->qhp/dot_general | solution.py:98
  247.3 0.7 copy-done
  248.5 16.4 %all-gather.5 = f32[4,1,256]{2,1,0:T(1,128)S(1)} all-gather(f32[1,1,256]{2,1,0:T(1,128)S(1)} %bitcast.233), channel_id=4, replica_groups=mesh['seq_0'=8,'seq_1'=4,'seq_2'=4,'tp'=4] {'tp'}, dimensions={0}, use_global_device_ids=true | all-gather | bytes 5120 | tf_op jit(solution)/shard_map/all_gather | solution.py:42
  265.0 1.3 multiply_convert_fusion
  (52 shorter events, 5.6 us)
Async XLA Ops:
  6.5 15.5 %copy-start.1 = (bf16[256,128]{1,0:T(8,128)(2,1)S(1)}, bf16[256,128]{1,0:T(8,128)(2,1)}, u32[]{:S(2)}) copy-start(bf16[256,128]{1,0:T(8,128)(2,1)} %param.13) | copy-start | bytes 196612
  6.5 64.0 %all-gather.14.cloned.1.call-start = ((), (), s32[]{:S(2)}) async-start(), calls=%async_computation.2 | async-start | bytes 3276800 | tf_op jit(solution)/shard_map/all_gather | solution.py:25
  7.3 14.7 %collective-permute-start.1 = (bf16[3,128]{1,0:T(4,128)(2,1)S(1)}, bf16[3,128]{1,0:T(4,128)(2,1)S(1)}, u32[]{:S(2)}, u32[]{:S(2)}) collective-permute-start(bf16[3,128]{1,0:T(4,128)(2,1)S(1)} %slice.203), channel_id=1, source_target_pairs={{0,4},{4,8},{8,12},{12,16},{16,20},{20,24},{24,28},{28,32},{32,36}... | collective-permute-start | bytes 2312 | tf_op jit(solution)/shard_map/ppermute | solution.py:38
  23.5 92.9 %all-gather.10.cloned.1.call-start = ((), (), s32[]{:S(2)}) async-start(), calls=%async_computation | async-start | bytes 3276800 | tf_op jit(solution)/shard_map/all_gather | solution.py:25
  73.3 167.7 %all-gather.12.cloned.1.call-start = ((), (), s32[]{:S(2)}) async-start(), calls=%async_computation.1 | async-start | bytes 5898240 | tf_op jit(solution)/shard_map/all_gather | solution.py:25
  116.4 2.8 %copy-start.2 = (bf16[256,128]{1,0:T(8,128)(2,1)S(1)}, bf16[256,128]{1,0:T(8,128)(2,1)}, u32[]{:S(2)}) copy-start(bf16[256,128]{1,0:T(8,128)(2,1)} %param.14) | copy-start | bytes 196612
  119.2 33.1 %collective-permute-start = (bf16[3,128]{1,0:T(4,128)(2,1)S(1)}, bf16[3,128]{1,0:T(4,128)(2,1)S(1)}, u32[]{:S(2)}, u32[]{:S(2)}) collective-permute-start(bf16[3,128]{1,0:T(4,128)(2,1)S(1)} %slice.193), channel_id=1, source_target_pairs={{0,4},{4,8},{8,12},{12,16},{16,20},{20,24},{24,28},{28,32},{32,36}... | collective-permute-start | bytes 2312 | tf_op jit(solution)/shard_map/ppermute | solution.py:38
  246.9 1.1 copy-start
  248.0 17.0 %copy-start.3 = (f32[1280]{0:T(1024)S(1)}, f32[1280]{0:T(1024)}, u32[]{:S(2)}) copy-start(f32[1280]{0:T(1024)} %param.20) | copy-start | bytes 15364
Sparse Core Ops, SparseCore 0:
  23.6 46.8 all-gather.13
  73.4 42.9 all-gather.9
  119.3 121.6 all-gather.11
where the time goes:
time: 273 us
  waiting for transfers between devices  160 us (59%)
  blocking collectives  61.7 us (23%)
  between operations  14.6 us (5%)
  other arithmetic  13.2 us (5%)
  matrix products  9.79 us (4%)
  starting transfers between devices  7.11 us (3%)
  local copies, waits for them, and re-layouts  6.55 us (2%)
    all_gather x3, waiting for transfers between devices, carried_in(): pieces = jax.tree.map(lambda part: lax.all_gather(part, axis), so_far)  160 us
    all_gather x3, blocking collectives, carried_in(): pieces = jax.tree.map(lambda part: lax.all_gather(part, axis), so_far)  45.3 us
    all_gather x1, blocking collectives, gathered_total(): parts = lax.all_gather(array, axis)  16.4 us
    ppermute x2, starting transfers between devices, from_behind(): lax.ppermute(value, axis, [(source, source + steps) for source in range(f...  7.02 us
    dot_general x1, matrix products, emit_rows(): jnp.einsum('qn,hpn->qhp', c_block, state_in.astype(jnp.bfloat16), preferr...  5.9 us
    add x2, other arithmetic, combine(): later[0][:, None, None] * earlier[1] + later[1]  5.57 us
  transfers between devices with their start and end apart: 5, of which 3 were waited for; matrix products, arithmetic and copies ran while one was open for 5% of the time, Pallas kernels for 0%

commit v1 on v0

v1 whole, which is shorter than its diff:
```python
import functools

import jax
import jax.numpy as jnp
from jax import lax
from jax.experimental import pallas as pl
from jax.experimental.pallas import tpu as pltpu
from jax.sharding import PartitionSpec as P

MESH = pl.DeviceIdType.MESH
EPS = 1e-05
SUPER = 32
HALVES = 2


def locate(position, doc_lengths):
    starts = (jnp.cumsum(doc_lengths) - doc_lengths).astype(jnp.int32)
    chosen = jnp.where(starts[None, :] <= position[:, None], starts[None, :], 0)
    return jnp.max(chosen, axis=1).astype(jnp.int32)


def convolve(padded, weight, conv_bias, position, doc_start):
    taps = weight.shape[0]
    tokens = position.shape[0]
    widened = padded.astype(jnp.float32)
    summed = jnp.broadcast_to(conv_bias[None, :], (tokens, conv_bias.shape[0]))
    for offset in range(taps):
        inside = (position - (taps - 1 - offset) >= doc_start)[:, None]
        summed = summed + jnp.where(
            inside, weight[offset][None, :] * widened[offset : offset + tokens], 0.0
        )
    return jax.nn.silu(summed).astype(jnp.bfloat16)


def carry_kernel(
    groups, e_ref, f_ref, q_ref, er, fr, tot, ztot, qs, qr, wide, fs, zfs,
    e_send, e_recv, f_send, f_recv, z_send, z_recv, zf_send, zf_recv, q_send, q_recv,
):
    me = lax.axis_index("seq")
    group, place = me // SUPER, me % SUPER
    dz, dy, dx = place // 16, (place // 4) % 4, place % 4
    rows, lanes = er.shape[1], er.shape[2]

    def partner(d):
        to = ((dz + d // 16) % 2) * 16 + ((dy + (d // 4) % 4) % 4) * 4 + (dx + d % 4) % 4
        return to, group * SUPER + to

    barrier = pltpu.get_barrier_semaphore()

    def greet(d, carry):
        pl.semaphore_signal(barrier, 1, device_id={"seq": partner(d)[1]}, device_id_type=MESH)
        return carry

    lax.fori_loop(1, SUPER, greet, 0)
    for k in range(1, groups):
        there = ((group + k) % groups) * SUPER + place
        pl.semaphore_signal(barrier, 1, device_id={"seq": there}, device_id_type=MESH)
    pl.semaphore_wait(barrier, SUPER - 1 + groups - 1)

    def f_copy(d):
        return pltpu.make_async_remote_copy(
            f_ref, fr.at[place], f_send.at[d], f_recv.at[d],
            device_id={"seq": partner(d)[1]}, device_id_type=MESH,
        )

    def e_copy(d):
        to = partner(d)[0]
        source = e_ref.at[
            pl.ds(pl.multiple_of((to // HALVES) * rows, 8), rows),
            pl.ds(pl.multiple_of((to % HALVES) * lanes, 128), lanes),
        ]
        return pltpu.make_async_remote_copy(
            source, er.at[place], e_send.at[d], e_recv.at[d],
            device_id={"seq": partner(d)[1]}, device_id_type=MESH,
        )

    def q_copy(d):
        to, there = partner(d)
        return pltpu.make_async_remote_copy(
            qs.at[to], qr.at[place], q_send.at[d], q_recv.at[d],
            device_id={"seq": there}, device_id_type=MESH,
        )

    def start_e(d, carry):
        f_copy(d).start()
        e_copy(d).start()
        return carry

    lax.fori_loop(1, SUPER, start_e, 0)
    fr[place] = f_ref[...]
    er[place] = e_ref[
        pl.ds(pl.multiple_of((place // HALVES) * rows, 8), rows),
        pl.ds(pl.multiple_of((place % HALVES) * lanes, 128), lanes),
    ]

    def wait_e(d, carry):
        f_copy(d).wait()
        e_copy(d).wait()
        return carry

    lax.fori_loop(1, SUPER, wait_e, 0)

    heads = f_ref.shape[1]
    width = lanes // 10
    column = lax.broadcasted_iota(jnp.int32, (heads, lanes), 1) // width + (place % HALVES) * 10
    pick = (column == lax.broadcasted_iota(jnp.int32, (heads, lanes), 0)).astype(jnp.float32)

    def expand(row):
        return jnp.dot(
            jnp.broadcast_to(row, (8, heads)), pick,
            precision=lax.Precision.HIGHEST, preferred_element_type=jnp.float32,
        )

    def spread(k, carry):
        fs[k] = expand(fr[k])
        return carry

    lax.fori_loop(0, SUPER, spread, 0)

    def total(k, pair):
        state, factor = pair
        return fs[k] * state + er[k], fr[k] * factor

    state, factor = lax.fori_loop(
        0, SUPER, total, (jnp.zeros((rows, lanes), jnp.float32), jnp.ones((1, heads), jnp.float32))
    )
    tot[...] = state
    zfs[...] = factor

    def z_copies(k):
        there = (group + k) * SUPER + place
        device = {"seq": there}
        return (
            pltpu.make_async_remote_copy(
                tot, ztot.at[pl.ds(group, 1)].at[0], z_send.at[k], z_recv.at[k],
                device_id=device, device_id_type=MESH,
            ),
            pltpu.make_async_remote_copy(
                zfs, wide.at[pl.ds(group, 1)].at[0], zf_send.at[k], zf_recv.at[k],
                device_id=device, device_id_type=MESH,
            ),
        )

    for k in range(1, groups):
        @pl.when(group + k < groups)
        def _():
            for copy in z_copies(k):
                copy.start()

    for k in range(1, groups):
        @pl.when(group - k >= 0)
        def _():
            for copy in z_copies(k):
                copy.wait_recv()

    er_in = jnp.zeros((rows, lanes), jnp.float32)
    for k in range(groups - 1):
        er_in = jnp.where(k < group, expand(wide[k]) * er_in + ztot[k], er_in)

    def emit(k, state):
        qs[k] = state.astype(jnp.bfloat16)
        return fs[k] * state + er[k]

    lax.fori_loop(0, SUPER, emit, er_in)

    def start_q(d, carry):
        q_copy(d).start()
        return carry

    lax.fori_loop(1, SUPER, start_q, 0)
    qr[place] = qs[place]

    for k in range(1, groups):
        @pl.when(group + k < groups)
        def _():
            for copy in z_copies(k):
                copy.wait_send()

    def wait_q(d, carry):
        q_copy(d).wait()
        return carry

    lax.fori_loop(1, SUPER, wait_q, 0)
    for k in range(0, SUPER // HALVES, 2):
        for half in range(HALVES):
            pair = [qr[(k + u) * HALVES + half].astype(jnp.float32) for u in range(2)]
            q_ref[k * rows : (k + 2) * rows, half * lanes : (half + 1) * lanes] = jnp.concatenate(
                pair, 0
            ).astype(jnp.bfloat16)


def carried(ends, factor, groups):
    state, features = ends.shape
    rows, lanes = state * HALVES // SUPER, features // HALVES
    f32 = jnp.float32
    dma = pltpu.SemaphoreType.DMA
    return pl.pallas_call(
        functools.partial(carry_kernel, groups),
        out_shape=jax.ShapeDtypeStruct((state, features), jnp.bfloat16),
        in_specs=[pl.BlockSpec(memory_space=pltpu.VMEM)] * 2,
        out_specs=pl.BlockSpec(memory_space=pltpu.VMEM),
        scratch_shapes=[
            pltpu.VMEM((SUPER, rows, lanes), f32),
            pltpu.VMEM((SUPER, 1, 128), f32),
            pltpu.VMEM((rows, lanes), f32),
            pltpu.VMEM((groups, rows, lanes), f32),
            pltpu.VMEM((SUPER, rows, lanes), jnp.bfloat16),
            pltpu.VMEM((SUPER, rows, lanes), jnp.bfloat16),
            pltpu.VMEM((groups, 1, 128), f32),
            pltpu.VMEM((SUPER, rows, lanes), f32),
            pltpu.VMEM((1, 128), f32),
            dma((SUPER,)), dma((SUPER,)), dma((SUPER,)), dma((SUPER,)),
            dma((groups,)), dma((groups,)), dma((groups,)), dma((groups,)),
            dma((SUPER,)), dma((SUPER,)),
        ],
        compiler_params=pltpu.CompilerParams(collective_id=0, has_side_effects=True),
    )(ends, factor)


def square_kernel(count, s_ref, o_ref, parts, send, recv):
    me = lax.axis_index("tp")
    barrier = pltpu.get_barrier_semaphore()
    for k in range(1, count):
        pl.semaphore_signal(
            barrier, 1, device_id={"tp": (me + k) % count}, device_id_type=MESH
        )
    pl.semaphore_wait(barrier, count - 1)
    copies = [
        pltpu.make_async_remote_copy(
            s_ref, parts.at[k - 1], send.at[k - 1], recv.at[k - 1],
            device_id={"tp": (me + k) % count}, device_id_type=MESH,
        )
        for k in range(1, count)
    ]
    for copy in copies:
        copy.start()
    for copy in copies:
        copy.wait()
    mine = [parts[k] for k in range(count - 1)]
    o_ref[...] = s_ref[...] + (mine[0] + mine[1] + mine[2])


def row_totals(sums, count):
    dma = pltpu.SemaphoreType.DMA
    shape = sums.shape
    return pl.pallas_call(
        functools.partial(square_kernel, count),
        out_shape=jax.ShapeDtypeStruct(shape, jnp.float32),
        in_specs=[pl.BlockSpec(memory_space=pltpu.VMEM)],
        out_specs=pl.BlockSpec(memory_space=pltpu.VMEM),
        scratch_shapes=[
            pltpu.VMEM((count - 1,) + shape, jnp.float32), dma((count - 1,)), dma((count - 1,)),
        ],
        compiler_params=pltpu.CompilerParams(collective_id=1, has_side_effects=True),
    )(sums)


def body(
    inputs, gate_input, b_source, c_source, step_raw, step_bias, decay_rate,
    conv_weight, conv_bias, norm_gain, doc_lengths,
):
    shards, parts = lax.axis_size("seq"), lax.axis_size("tp")
    tokens = inputs.shape[0]
    heads = step_raw.shape[1]
    width = inputs.shape[1] // heads
    state = b_source.shape[1]
    keep = conv_weight.shape[0] - 1
    f32 = jnp.float32
    position = lax.axis_index("seq") * tokens + jnp.arange(tokens, dtype=jnp.int32)
    doc_start = locate(position, doc_lengths)
    source = jnp.concatenate([b_source, c_source], 1)
    before = lax.ppermute(
        source[tokens - keep :], "seq", [(k, k + 1) for k in range(shards - 1)]
    )
    conv = convolve(
        jnp.concatenate([before, source], 0), conv_weight, conv_bias, position, doc_start
    )
    b_conv, c_conv = conv[:, :state], conv[:, state:]
    step = jax.nn.softplus(step_raw + step_bias[None, :])
    cumulated = jnp.cumsum(-step * decay_rate[None, :], axis=0)
    same = (doc_start == doc_start[-1])[:, None]
    weighting = jnp.where(same, jnp.exp(cumulated[-1][None, :] - cumulated) * step, 0.0)
    weighted = (
        inputs.reshape(tokens, heads, width).astype(f32) * weighting[:, :, None]
    ).astype(jnp.bfloat16).reshape(tokens, heads * width)
    ends = lax.dot_general(
        b_conv, weighted, (((0,), (0,)), ((), ())), preferred_element_type=f32
    )
    factor = jnp.where(doc_start[-1] < position[0], jnp.exp(cumulated[-1]), 0.0)
    factor = jnp.concatenate([factor, jnp.zeros((128 - heads,), f32)])[None, :]
    q = carried(ends, factor, shards // SUPER)

    products = jnp.dot(c_conv, b_conv.T, preferred_element_type=f32)
    order = jnp.arange(tokens)
    causal = (order[None, :] <= order[:, None]) & (doc_start[None, :] == doc_start[:, None])
    gap = cumulated.T[:, :, None] - cumulated.T[:, None, :]
    scores = jnp.where(causal[None], products[None] * jnp.exp(gap) * step.T[:, None, :], 0.0)
    diagonal = jnp.einsum(
        "hts,shp->thp", scores.astype(jnp.bfloat16), inputs.reshape(tokens, heads, width),
        preferred_element_type=f32,
    )
    out_decay = jnp.where((doc_start < position[0])[:, None], jnp.exp(cumulated), 0.0)
    from_state = jnp.dot(c_conv, q, preferred_element_type=f32).reshape(tokens, heads, width)
    mixed = (diagonal + from_state * out_decay[:, :, None]).reshape(tokens, heads * width)
    gated = mixed * jax.nn.silu(gate_input.astype(f32))
    sums = jnp.sum(gated * gated, axis=1).reshape(tokens // 128, 128)
    mean_square = row_totals(sums, parts).reshape(tokens) / (heads * width * parts)
    return (gated * lax.rsqrt(mean_square + EPS)[:, None] * norm_gain[None, :]).astype(
        jnp.bfloat16
    )


def solution(mesh):
    both, seq = P("seq", "tp"), P("seq", None)
    return jax.shard_map(
        body, mesh=mesh,
        in_specs=(both, both, seq, seq, both, P("tp"), P("tp"), P(), P(), P("tp"), P()),
        out_specs=both, check_vma=False,
    )
```

time: 273 us -> 89.2 us (0.33)
  waiting for transfers between devices: 160 us -> 0.01 us
  blocking collectives: 61.7 us -> 0 us
  Pallas kernels: 0 us -> 61.4 us
  between operations: 14.6 us -> 1.59 us
  matrix products: 9.79 us -> 4.13 us
  starting transfers between devices: 7.11 us -> 3.94 us
  other arithmetic: 13.2 us -> 10.1 us
    all_gather x3 -> x0, waiting for transfers between devices: 160 us -> none  [carried_in(): pieces = jax.tree.map(lambda part: lax.all_gather(part, axis), so_far)]
    all_gather x4 -> x0, blocking collectives: 61.7 us -> none  [the longest x3 45.3 us: carried_in(): pieces = jax.tree.map(lambda part: lax.all_gather(part, axis), so_far)]
    pallas_call x0 -> x2, Pallas kernels: none -> 61.4 us  [the longest x1 47 us: carried(): pl.pallas_call(functools.partial(carry_kernel, groups), out_shape=jax.Sha...]
    dot_general x4, matrix products: 9.79 us -> 4.13 us  [the longest x1 1.38 us: body(): jnp.dot(c_conv, q, preferred_element_type=f32).reshape(tokens, heads, width)]
    add x3 -> x1, other arithmetic: 5.57 us -> 0.01 us  [body(): lax.axis_index('seq') * tokens + jnp.arange(tokens, dtype=jnp.int32)]
    ppermute x2 -> x1, starting transfers between devices: 7.02 us -> 3.94 us  [body(): lax.ppermute(source[tokens - keep:], 'seq', [(k, k + 1) for k in range(sh...]
  transfers between devices with their start and end apart: 5 -> 1, of which waited for: 3 -> 0; matrix products, arithmetic and copies ran while one was open for 5% -> 11% of each run, Pallas kernels for 0% -> 0%
where the time goes in v1:
time: 89.2 us; the launch traced here: 87.4 us
  Pallas kernels  61.4 us (69%)
  other arithmetic  10.1 us (11%)
  local copies, waits for them, and re-layouts  6.33 us (7%)
  matrix products  4.13 us (5%)
  starting transfers between devices  3.94 us (4%)
  between operations  1.59 us (2%)
    pallas_call x1, Pallas kernels, carried(): pl.pallas_call(functools.partial(carry_kernel, groups), out_shape=jax.Sha...  47 us
    pallas_call x1, Pallas kernels, row_totals(): pl.pallas_call(functools.partial(square_kernel, count), out_shape=jax.Sha...  14.4 us
    ppermute x1, starting transfers between devices, body(): lax.ppermute(source[tokens - keep:], 'seq', [(k, k + 1) for k in range(sh...  3.94 us
    unnamed x22, local copies, waits for them, and re-layouts  2.13 us
  transfers between devices with their start and end apart: 1, of which 0 were waited for; matrix products, arithmetic and copies ran while one was open for 11% of the time, Pallas kernels for 0%

profile of v1, /device:TPU:1, one launch (start us, length us, event | category | flops | bytes accessed | tf_op | source)
XLA Modules:
  0.0 87.4 jit_solution(3221570942480585658)
XLA Ops:
  0.0 0.9 %constant_dynamic-update-slice_fusion.1 = bf16[256,256]{1,0:T(8,128)(2,1)S(1)} fusion(bf16[256,128]{1,0:T(8,128)(2,1)} %param.13), kind=kLoop, calls=%fused_computation.52 | loop fusion | bytes 131072
  0.9 0.9 constant_dynamic-update-slice_fusion
  1.8 3.9 %collective-permute-start = (bf16[3,256]{1,0:T(4,128)(2,1)S(1)}, bf16[3,256]{1,0:T(4,128)(2,1)S(1)}, u32[]{:S(2)}, u32[]{:S(2)}) collective-permute-start(bf16[3,256]{1,0:T(4,128)(2,1)S(1)} %slice.67), channel_id=1, source_target_pairs={{0,4},{4,8},{8,12},{12,16},{16,20},{20,24},{24,28},{28,32},{32,36}... | collective-permute-start | bytes 4616 | tf_op jit(solution)/shard_map/ppermute | solution.py:272
  5.8 0.8 reduce-window.19
  6.6 0.7 bitcast_subtract_fusion
  7.2 0.5 slice.66
  7.8 0.7 slice.64
  9.9 1.3 %broadcast_compare_fusion = (pred[256]{0:T(512)(128)(4,1)S(1)}, pred[256]{0:T(512)(128)(4,1)S(1)}, pred[256]{0:T(512)(128)(4,1)S(1)}, pred[256]{0:T(512)(128)(4,...) fusion(s32[256]{0:T(256)S(1)} %select_reduce_fusion, s32[]{:T(128)} %bitcast.13, s32[]{:T(128)} %bitcast.10, ...), kind=kLoop, calls=%fused_computation.61 | loop fusion | flops 2560 | bytes 2572 | tf_op jit(solution)/shard_map/lt | solution.py:302
  11.2 0.7 fusion.22
  11.9 0.8 fusion.33
  12.8 0.8 multiply_bitcast_fusion
  13.6 0.6 reduce-window.20
  14.8 1.4 %multiply_select_fusion = (f32[256,20]{0,1:T(8,128)S(1)}, f32[20,256]{1,0:T(8,128)}, f32[256,20]{0,1:T(8,128)}) fusion(f32[20]{0:T(128)S(1)} %slice_reduce_fusion.1, pred[256]{0:T(512)(128)(4,1)S(1)} %get-tuple-element.13, f32[20,256]{1,0:T(8,128)S(1)} %bitcast.43, f32[256,20]{0,1:T(8,128)} %param.15, f32[20]{0:T(128)} %param.16, ...), kind=kLoop, calls=%fused_computation.46 | loop fusion | flops 56320 | bytes 103072 | tf_op jit(solution)/shard_map/jit(_where)/select_n | solution.py:282
  16.2 0.5 pad_bitcast_fusion.f_ref
  17.9 1.2 %fusion.23.e_ref = f32[128,1280]{1,0:T(8,128)} fusion(bf16[256,1280]{0,1:T(8,128)(2,1)S(1)} %fusion.13, bf16[256,256]{1,0:T(8,128)(2,1)S(1)} %multiply_convert_fusion.1), kind=kOutput, calls=%fused_computation.37 | convolution fusion | flops 83886080 | bytes 1376256 | tf_op jit(solution)/shard_map/dot_general | solution.py:286
  19.1 47.0 %shard_map.109 = bf16[128,1280]{1,0:T(8,128)(2,1)} custom-call(f32[128,1280]{1,0:T(8,128)} %fusion.23.e_ref, f32[1,128]{1,0:T(1,128)} %pad_bitcast_fusion.f_ref), custom_call_target="tpu_custom_call" | custom-call | tf_op jit(solution)/shard_map/pallas_call | solution.py:197
  66.1 1.4 %fusion.27 = f32[256,1280]{0,1:T(8,128)S(1)} fusion(bf16[128,1280]{1,0:T(8,128)(2,1)} %shard_map.109, bf16[256,256]{1,0:T(8,128)(2,1)S(1)} %multiply_convert_fusion.1), kind=kOutput, calls=%fused_computation.41 | convolution fusion | flops 83886080 | bytes 1703936 | tf_op jit(solution)/shard_map/dot_general | solution.py:303
  67.6 1.3 %fusion.8 = f32[256,20,64]{0,2,1:T(8,128)S(1)} fusion(bf16[256,20,64]{0,2,1:T(8,128)(2,1)S(1)} %bitcast.39, f32[20,256]{1,0:T(8,128)S(1)} %copy-done.5, f32[20,256]{1,0:T(8,128)S(1)} %bitcast.44, f32[256,256]{1,0:T(8,128)S(1)} %fusion.25, pred[256,256]{1,0:T(8,128)(4,1)S(1)} %copy-done.4, f32[256,20,64]{0,2,1:T(8,128)S(1)} %bitcast.41, ...), kind=kOutput, calls=%fused_computation.11 | convolution fusion | flops 174981120 | bytes 3665920 | tf_op jit(solution)/shard_map/hts,shp->thp/dot_general | solution.py:298
  68.9 0.4 copy.28
  69.3 0.7 copy-done
  70.0 1.1 %multiply_reduce_fusion = f32[256]{0:T(256)} fusion(f32[256,1280]{1,0:T(8,128)S(1)} %copy.28, bf16[256,1280]{1,0:T(8,128)(2,1)S(1)} %copy-done), kind=kLoop, calls=%fused_computation.19 | loop fusion | flops 2621184 | bytes 1967104 | tf_op jit(solution)/shard_map/reduce_sum | solution.py:306
  71.1 14.4 %shard_map.110 = f32[2,128]{1,0:T(2,128)} custom-call(f32[2,128]{1,0:T(2,128)} %bitcast.46), custom_call_target="tpu_custom_call" | custom-call | tf_op jit(solution)/shard_map/pallas_call | solution.py:246
  85.4 0.7 rsqrt_bitcast_fusion
  86.1 1.3 %multiply_convert_fusion = bf16[256,1280]{1,0:T(8,128)(2,1)} fusion(f32[1280]{0:T(1024)S(1)} %copy-done.7, f32[256]{0:T(256)S(1)} %rsqrt_bitcast_fusion, f32[256,1280]{1,0:T(8,128)S(1)} %copy.28, bf16[256,1280]{1,0:T(8,128)(2,1)S(1)} %copy-done), kind=kLoop, calls=%fused_computation.18 | loop fusion | flops 2949120 | bytes 2627584 | tf_op jit(solution)/shard_map/convert_element_type | solution.py:308
  (37 shorter events, 1.7 us)
Async XLA Ops:
  0.0 16.8 %copy-start.1 = (bf16[256,1280]{1,0:T(8,128)(2,1)S(1)}, bf16[256,1280]{1,0:T(8,128)(2,1)}, u32[]{:S(2)}) copy-start(bf16[256,1280]{1,0:T(8,128)(2,1)} %param.11) | copy-start | bytes 1966084
  1.8 15.3 %collective-permute-start = (bf16[3,256]{1,0:T(4,128)(2,1)S(1)}, bf16[3,256]{1,0:T(4,128)(2,1)S(1)}, u32[]{:S(2)}, u32[]{:S(2)}) collective-permute-start(bf16[3,256]{1,0:T(4,128)(2,1)S(1)} %slice.67), channel_id=1, source_target_pairs={{0,4},{4,8},{8,12},{12,16},{16,20},{20,24},{24,28},{28,32},{32,36}... | collective-permute-start | bytes 4616 | tf_op jit(solution)/shard_map/ppermute | solution.py:272
  14.6 1.6 %copy-start.2 = (f32[3,8,2,128]{3,1,2,0:T(8,128)}, f32[3,8,2,128]{3,1,2,0:T(8,128)S(1)}, u32[]{:S(2)}) copy-start(f32[3,8,2,128]{3,1,2,0:T(8,128)S(1)} %copy.30) | copy-start | bytes 73732
  16.8 0.7 copy-start.8
  66.1 1.4 %copy-start.3 = (f32[3,8,2,128]{3,1,2,0:T(8,128)S(1)}, f32[3,8,2,128]{3,1,2,0:T(8,128)}, u32[]{:S(2)}) copy-start(f32[3,8,2,128]{3,1,2,0:T(8,128)} %copy-done.2) | copy-start | bytes 73732
  66.1 1.4 %copy-start.4 = (pred[256,256]{1,0:T(8,128)(4,1)S(1)}, pred[256,256]{1,0:T(8,128)(4,1)}, u32[]{:S(2)}) copy-start(pred[256,256]{1,0:T(8,128)(4,1)} %fusion.22) | copy-start | bytes 196612
  66.1 1.4 %copy-start.5 = (f32[20,256]{1,0:T(8,128)S(1)}, f32[20,256]{1,0:T(8,128)}, u32[]{:S(2)}) copy-start(f32[20,256]{1,0:T(8,128)} %get-tuple-element.6) | copy-start | bytes 61444
  66.1 1.4 %copy-start.6 = (f32[256,20]{0,1:T(8,128)S(1)}, f32[256,20]{0,1:T(8,128)}, u32[]{:S(2)}) copy-start(f32[256,20]{0,1:T(8,128)} %get-tuple-element.7) | copy-start | bytes 61444
  68.9 1.1 %copy-start = (bf16[256,1280]{1,0:T(8,128)(2,1)S(1)}, bf16[256,1280]{1,0:T(8,128)(2,1)}, u32[]{:S(2)}) copy-start(bf16[256,1280]{1,0:T(8,128)(2,1)} %param.12) | copy-start | bytes 1966084
  70.0 16.1 %copy-start.7 = (f32[1280]{0:T(1024)S(1)}, f32[1280]{0:T(1024)}, u32[]{:S(2)}) copy-start(f32[1280]{0:T(1024)} %param.20) | copy-start | bytes 15364

commit v2 on v0

v2 whole, which is shorter than its diff:
```python
import functools

import jax
import jax.numpy as jnp
from jax import lax
from jax.experimental import pallas as pl
from jax.experimental.pallas import tpu as pltpu
from jax.sharding import PartitionSpec as P

MESH = pl.DeviceIdType.MESH
EPS = 1e-05
SUPER = 32
F32 = jnp.float32
BF16 = jnp.bfloat16
EXACT = lax.Precision.HIGHEST


def remote(source, target, send, recv, **device):
    return pltpu.make_async_remote_copy(
        source, target, send, recv, device_id=device, device_id_type=MESH
    )


def layer_kernel(
    groups, parts, heads,
    x_hbm, gate_hbm, b_ref, c_ref, step_ref, bias_ref, rate_ref, taps_ref, shift_ref, gain_ref,
    docs_ref, out_ref,
    x, gate, steps, ext, halo, weighted, c_conv, rows_c, factor, ends, er, fr, wide,
    carry_in, carry_out, qs, qr, q, dg, rs, sums, others,
    x_sem, h_send, h_recv, f_send, f_recv, e_send, e_recv, z_send, z_recv, q_send, q_recv,
    s_send, s_recv,
):
    me, part = lax.axis_index("seq"), lax.axis_index("tp")
    shards = groups * SUPER
    group, place = me // SUPER, me % SUPER
    dz, dy, dx = place // 16, (place // 4) % 4, place % 4
    tokens, features = x.shape
    state = b_ref.shape[1]
    rows, lanes = er.shape[1], er.shape[2]
    width = features // heads
    pairs = features // 128

    def partner(d):
        to = ((dz + d // 16) % 2) * 16 + ((dy + (d // 4) % 4) % 4) * 4 + (dx + d % 4) % 4
        return to, group * SUPER + to

    def each(f):
        def step(d, carry):
            f(d)
            return carry

        lax.fori_loop(1, SUPER, step, 0)

    x_in = pltpu.make_async_copy(x_hbm, x, x_sem.at[0])
    gate_in = pltpu.make_async_copy(gate_hbm, gate, x_sem.at[1])
    x_in.start()
    gate_in.start()

    barrier = pltpu.get_barrier_semaphore()

    def signal(**device):
        pl.semaphore_signal(barrier, 1, device_id=device, device_id_type=MESH)

    each(lambda d: signal(seq=partner(d)[1]))
    for k in range(1, parts):
        signal(tp=(part + k) % parts)
    has_next, has_last = group + 1 < groups, group > 0
    ends_group, opens_group = place == SUPER - 1, place == 0
    pl.when(has_next)(lambda: signal(seq=me + SUPER))
    pl.when(has_last)(lambda: signal(seq=me - SUPER))
    pl.when(has_next & ends_group)(lambda: signal(seq=me + 1))
    pl.when(has_last & opens_group)(lambda: signal(seq=me - 1))

    first = me * tokens
    starts, at = [], jnp.int32(0)
    for k in range(docs_ref.shape[0]):
        starts.append(at)
        at = at + docs_ref[k]

    def locate(position):
        found = jnp.zeros_like(position)
        for start in starts:
            found = jnp.maximum(found, jnp.where(position >= start, start, 0))
        return found

    position = first + lax.broadcasted_iota(jnp.int32, (tokens, 128), 0)
    doc = locate(position)
    doc_row = locate(first + lax.broadcasted_iota(jnp.int32, (8, tokens), 1))
    doc_last = doc_row[0:1, tokens - 1 : tokens]

    steps[...] = jnp.zeros_like(steps)
    steps[:, :heads] = jax.nn.softplus(step_ref[...] + bias_ref[...])
    rates = jnp.concatenate([rate_ref[...], jnp.zeros((1, 128 - heads), F32)], 1)
    log_decay = -steps[...] * rates
    order = lax.broadcasted_iota(jnp.int32, (tokens, tokens), 0)
    across = lax.broadcasted_iota(jnp.int32, (tokens, tokens), 1)
    lower = across <= order
    cumulated = jnp.dot(
        lower.astype(F32), log_decay, precision=EXACT, preferred_element_type=F32
    )
    grown = jnp.exp(cumulated)
    shrunk = jnp.exp(-cumulated) * steps[...]
    last = grown[tokens - 1 : tokens, :]
    rows_c[...] = shrunk.T
    weights = jnp.where(doc == doc_last, shrunk * last, 0.0)
    opened = jnp.where(doc < first, grown, 0.0)
    factor[...] = opened[tokens - 1 : tokens, :]

    count = (
        SUPER - 1 + parts - 1 + has_next.astype(jnp.int32) + has_last.astype(jnp.int32)
        + (has_next & ends_group).astype(jnp.int32) + (has_last & opens_group).astype(jnp.int32)
    )
    pl.semaphore_wait(barrier, count)

    def halo_copies():
        return [
            remote(
                ref.at[pl.ds(tokens - 16, 16), :], halo.at[k], h_send.at[k], h_recv.at[k],
                seq=me + 1,
            )
            for k, ref in enumerate((b_ref, c_ref))
        ]

    @pl.when(me + 1 < shards)
    def _():
        for copy in halo_copies():
            copy.start()

    def f_copy(d):
        return remote(factor, fr.at[place], f_send.at[d], f_recv.at[d], seq=partner(d)[1])

    def e_copy(d):
        to, there = partner(d)
        source = ends.at[
            pl.ds(pl.multiple_of((to % 16) * rows, 8), rows),
            pl.ds(pl.multiple_of((to // 16) * lanes, 128), lanes),
        ]
        return remote(source, er.at[place], e_send.at[d], e_recv.at[d], seq=there)

    def q_copy(d):
        to, there = partner(d)
        return remote(qs.at[to], qr.at[place], q_send.at[d], q_recv.at[d], seq=there)

    each(lambda d: f_copy(d).start())

    low = lax.broadcasted_iota(jnp.int32, (tokens, 128), 1) < width

    def spread(columns, pair):
        one = jnp.broadcast_to(columns[:, 2 * pair : 2 * pair + 1], (tokens, 128))
        two = jnp.broadcast_to(columns[:, 2 * pair + 1 : 2 * pair + 2], (tokens, 128))
        return jnp.where(low, one, two)

    x_in.wait()
    for pair in range(pairs):
        cut = slice(128 * pair, 128 * pair + 128)
        weighted[:, cut] = (x[:, cut].astype(F32) * spread(weights, pair)).astype(BF16)

    ext[8:, :state] = b_ref[...].astype(F32)
    ext[8:, state:] = c_ref[...].astype(F32)

    @pl.when(me > 0)
    def _():
        for copy in halo_copies():
            copy.wait_recv()

    @pl.when(me == 0)
    def _():
        halo[...] = jnp.zeros_like(halo)

    ext[:8, :state] = halo[0].astype(F32)[8:]
    ext[:8, state:] = halo[1].astype(F32)[8:]

    def convolve(half):
        cut = slice(half * state, half * state + state)
        total = jnp.broadcast_to(shift_ref[:, cut], (tokens, state))
        for k in range(4):
            back = 3 - k
            term = taps_ref[k : k + 1, cut] * ext[8 - back : 8 - back + tokens, cut]
            total = total + jnp.where(position - back >= doc, term, 0.0)
        return total * jax.nn.sigmoid(total)

    b_turned = convolve(0).T.astype(BF16)
    ends[...] = jnp.dot(b_turned, weighted[...], preferred_element_type=F32)
    each(lambda d: e_copy(d).start())
    fr[place] = factor[...]
    er[place] = ends[
        pl.ds(pl.multiple_of((place % 16) * rows, 8), rows),
        pl.ds(pl.multiple_of((place // 16) * lanes, 128), lanes),
    ]

    c_conv[...] = convolve(1).astype(BF16)
    products = jnp.dot(c_conv[...], b_turned, preferred_element_type=F32)
    doc_wide = jnp.concatenate([doc, doc], 1)
    products = jnp.where(lower & (doc_row[0:1, :] == doc_wide), products, 0.0)
    half = tokens // 2
    top, bottom = products[:half, :half], products[half:, :]
    gate_in.wait()
    for pair in range(pairs):
        cut = slice(128 * pair, 128 * pair + 128)
        found = []
        for h in (2 * pair, 2 * pair + 1):
            decay = jnp.broadcast_to(grown[:, h : h + 1], (tokens, 128))
            row = rows_c[h : h + 1, :]
            low_scores = top * row[:, :half] * decay[:half]
            high = jnp.concatenate([decay[half:], decay[half:]], 1)
            high_scores = bottom * row * high
            found.append(
                jnp.concatenate(
                    [
                        jnp.dot(
                            low_scores.astype(BF16), x[:half, cut], preferred_element_type=F32
                        ),
                        jnp.dot(
                            high_scores.astype(BF16), x[:, cut], preferred_element_type=F32
                        ),
                    ],
                    0,
                )
            )
        opening = gate[:, cut].astype(F32)
        opening = opening * jax.nn.sigmoid(opening)
        dg[:, cut] = jnp.where(low, found[0], found[1]) * opening
        rs[:, cut] = spread(opened, pair) * opening

    each(lambda d: f_copy(d).wait())
    column = lax.broadcasted_iota(jnp.int32, (128, lanes), 1) // width
    column = column + (place // 16) * (lanes // width)
    pick = (column == lax.broadcasted_iota(jnp.int32, (128, lanes), 0)).astype(F32)
    gathered = jnp.concatenate([fr[k] for k in range(SUPER)], 0)
    wide[...] = jnp.dot(gathered, pick, precision=EXACT, preferred_element_type=F32)
    each(lambda d: e_copy(d).wait())

    def factor_of(k):
        return jnp.broadcast_to(wide[k : k + 1, :], (rows, lanes))

    total, scale = er[0], factor_of(0)
    for k in range(1, SUPER):
        total = factor_of(k) * total + er[k]
        scale = factor_of(k) * scale

    def z_copy():
        return remote(carry_out, carry_in, z_send, z_recv, seq=me + SUPER)

    @pl.when(has_last)
    def _():
        z_copy().wait_recv()

    @pl.when(group == 0)
    def _():
        carry_in[...] = jnp.zeros_like(carry_in)

    current = carry_in[...]
    carry_out[...] = scale * current + total

    @pl.when(has_next)
    def _():
        z_copy().start()

    for k in range(SUPER):
        qs[k] = current.astype(BF16)
        if k + 1 < SUPER:
            current = factor_of(k) * current + er[k]
    each(lambda d: q_copy(d).start())
    qr[place] = qs[place]

    @pl.when(has_next)
    def _():
        z_copy().wait_send()

    @pl.when(me + 1 < shards)
    def _():
        for copy in halo_copies():
            copy.wait_send()

    each(lambda d: q_copy(d).wait())
    for side in range(2):
        for k in range(0, 16, 2):
            both = [qr[side * 16 + k + u].astype(F32) for u in range(2)]
            q[k * rows : (k + 2) * rows, side * lanes : (side + 1) * lanes] = jnp.concatenate(
                both, 0
            ).astype(BF16)

    squares = jnp.zeros((tokens, 128), F32)
    for pair in range(pairs):
        cut = slice(128 * pair, 128 * pair + 128)
        from_state = jnp.dot(c_conv[...], q[:, cut], preferred_element_type=F32)
        gated = dg[:, cut] + from_state * rs[:, cut]
        dg[:, cut] = gated
        squares = squares + gated * gated
    sums[...] = jnp.sum(squares.T, axis=0, keepdims=True)
    copies = [
        remote(sums, others.at[k - 1], s_send.at[k - 1], s_recv.at[k - 1], tp=(part + k) % parts)
        for k in range(1, parts)
    ]
    for copy in copies:
        copy.start()
    for copy in copies:
        copy.wait()
    mean_square = (sums[...] + others[0] + others[1] + others[2]) * (1.0 / (features * parts))
    inverse = lax.rsqrt(mean_square + EPS)
    inverse = jnp.broadcast_to(inverse, (128, tokens)).T
    for pair in range(pairs):
        cut = slice(128 * pair, 128 * pair + 128)
        out_ref[:, cut] = (dg[:, cut] * inverse * gain_ref[:, cut]).astype(BF16)


def body(
    inputs, gate_input, b_source, c_source, step_raw, step_bias, decay_rate,
    conv_weight, conv_bias, norm_gain, doc_lengths,
):
    groups, parts = lax.axis_size("seq") // SUPER, lax.axis_size("tp")
    tokens, features = inputs.shape
    heads, state = step_raw.shape[1], b_source.shape[1]
    rows, lanes = state // 16, features // 2
    dma = pltpu.SemaphoreType.DMA
    vmem = pltpu.VMEM
    whole = pl.BlockSpec(memory_space=pltpu.VMEM)
    far = pl.BlockSpec(memory_space=pl.ANY)
    return pl.pallas_call(
        functools.partial(layer_kernel, groups, parts, heads),
        out_shape=jax.ShapeDtypeStruct((tokens, features), BF16),
        in_specs=[far, far] + [whole] * 8 + [pl.BlockSpec(memory_space=pltpu.SMEM)],
        out_specs=whole,
        scratch_shapes=[
            vmem((tokens, features), BF16),
            vmem((tokens, features), BF16),
            vmem((tokens, 128), F32),
            vmem((8 + tokens, 2 * state), F32),
            vmem((2, 16, state), BF16),
            vmem((tokens, features), BF16),
            vmem((tokens, state), BF16),
            vmem((128, tokens), F32),
            vmem((1, 128), F32),
            vmem((state, features), F32),
            vmem((SUPER, rows, lanes), F32),
            vmem((SUPER, 1, 128), F32),
            vmem((SUPER, lanes), F32),
            vmem((rows, lanes), F32),
            vmem((rows, lanes), F32),
            vmem((SUPER, rows, lanes), BF16),
            vmem((SUPER, rows, lanes), BF16),
            vmem((state, features), BF16),
            vmem((tokens, features), F32),
            vmem((tokens, features), F32),
            vmem((1, tokens), F32),
            vmem((parts - 1, 1, tokens), F32),
            dma((2,)), dma((2,)), dma((2,)), dma((SUPER,)), dma((SUPER,)), dma((SUPER,)),
            dma((SUPER,)), dma, dma, dma((SUPER,)), dma((SUPER,)),
            dma((parts - 1,)), dma((parts - 1,)),
        ],
        compiler_params=pltpu.CompilerParams(
            collective_id=0, has_side_effects=True, vmem_limit_bytes=48 * 1024 * 1024
        ),
    )(
        inputs, gate_input, b_source, c_source, step_raw, step_bias[None, :],
        decay_rate[None, :], conv_weight, conv_bias[None, :], norm_gain[None, :], doc_lengths,
    )


def solution(mesh):
    both, seq = P("seq", "tp"), P("seq", None)
    return jax.shard_map(
        body, mesh=mesh,
        in_specs=(both, both, seq, seq, both, P("tp"), P("tp"), P(), P(), P("tp"), P()),
        out_specs=both, check_vma=False,
    )
```

time: 273 us -> 58.7 us (0.22)
  the two profiles are of different devices: /device:TPU:1 before, /device:TPU:481 now
where the time goes in v2:
time: 58.7 us; the launch traced here: 58.4 us
  Pallas kernels  53.6 us (91%)
  local copies, waits for them, and re-layouts  4.67 us (8%)
    pallas_call x1, Pallas kernels, body(): pl.pallas_call(functools.partial(layer_kernel, groups, parts, heads), out...  53.6 us
    unnamed x20, local copies, waits for them, and re-layouts  3.97 us

profile of v2, /device:TPU:481, one launch (start us, length us, event | category | flops | bytes accessed | tf_op | source)
XLA Modules:
  0.0 58.4 jit_solution(9612446628324579119)
XLA Ops:
  0.0 0.7 %broadcast_in_dim.15.gain_ref = f32[1,1280]{1,0:T(1,128)S(1)} reshape(f32[1280]{0:T(1024)} %param.20) | data formatting | bytes 10240 | tf_op jit(solution)/shard_map/broadcast_in_dim | solution.py:356
  0.7 0.0 copy-start.2
  0.7 0.0 copy-start.3
  0.7 0.0 copy-start.4
  0.7 0.0 copy-start.5
  0.7 0.0 copy-start.6
  0.7 0.0 copy-start.7
  0.7 0.0 copy-start.8
  0.8 0.9 %copy.12.step_ref = f32[256,20]{1,0:T(8,128)S(1)} copy(f32[256,20]{0,1:T(8,128)} %param.15) | data formatting | bytes 40960 | tf_op args[4]
  1.7 0.0 copy-done.2
  1.7 0.0 copy-done.3
  1.7 0.0 copy-done.4
  1.7 0.0 copy-done.5
  1.7 0.0 copy-done.6
  1.7 0.0 copy-done.7
  1.7 0.0 copy-done.8
  1.8 0.0 copy-start
  1.8 1.1 %copy-done = bf16[256,1280]{1,0:T(8,128)(2,1)S(1)} copy-done((bf16[256,1280]{1,0:T(8,128)(2,1)S(1)}, bf16[256,1280]{1,0:T(8,128)(2,1)}, u32[]{:S(2)}) %copy-start) | copy-done | bytes 655384
  2.8 0.0 copy-start.1
  2.8 1.1 %copy-done.1 = bf16[256,1280]{1,0:T(8,128)(2,1)S(1)} copy-done((bf16[256,1280]{1,0:T(8,128)(2,1)S(1)}, bf16[256,1280]{1,0:T(8,128)(2,1)}, u32[]{:S(2)}) %copy-start.1) | copy-done | bytes 655384
  3.9 53.6 %shard_map.109 = bf16[256,1280]{1,0:T(8,128)(2,1)S(1)} custom-call(bf16[256,1280]{1,0:T(8,128)(2,1)S(1)} %copy-done, bf16[256,1280]{1,0:T(8,128)(2,1)S(1)} %copy-done.1, bf16[256,128]{1,0:T(8,128)(2,1)S(1)} %copy-done.2, bf16[256,128]{1,0:T(8,128)(2,1)S(1)} %copy-done.3, f32[256,20]{1,0:T(8,128)S(1)} %copy.12.step_ref, f32[1,20]{1,0:T(1,128)S(1)} %bitcast.4, ...), custom_call_target="tpu_custom_call" | custom-call | tf_op jit(solution)/shard_map/pallas_call | solution.py:319
  57.6 0.8 %copy.14 = bf16[256,1280]{1,0:T(8,128)(2,1)} copy(bf16[256,1280]{1,0:T(8,128)(2,1)S(1)} %shard_map.109) | data formatting | bytes 1310720
Async XLA Ops:
  0.7 1.0 %copy-start.2 = (bf16[256,128]{1,0:T(8,128)(2,1)S(1)}, bf16[256,128]{1,0:T(8,128)(2,1)}, u32[]{:S(2)}) copy-start(bf16[256,128]{1,0:T(8,128)(2,1)} %b_ref.1) | copy-start | bytes 196612
  0.7 1.0 %copy-start.3 = (bf16[256,128]{1,0:T(8,128)(2,1)S(1)}, bf16[256,128]{1,0:T(8,128)(2,1)}, u32[]{:S(2)}) copy-start(bf16[256,128]{1,0:T(8,128)(2,1)} %c_ref.1) | copy-start | bytes 196612
  0.7 1.0 %copy-start.4 = (f32[4,256]{1,0:T(4,128)S(1)}, f32[4,256]{1,0:T(4,128)}, u32[]{:S(2)}) copy-start(f32[4,256]{1,0:T(4,128)} %taps_ref.1) | copy-start | bytes 12292
  0.7 1.0 %copy-start.5 = (f32[256]{0:T(256)S(1)}, f32[256]{0:T(256)}, u32[]{:S(2)}) copy-start(f32[256]{0:T(256)} %param.19) | copy-start | bytes 3076
  0.7 1.0 %copy-start.6 = (f32[20]{0:T(128)S(1)}, f32[20]{0:T(128)}, u32[]{:S(2)}) copy-start(f32[20]{0:T(128)} %param.16) | copy-start | bytes 244
  0.7 1.0 %copy-start.7 = (f32[20]{0:T(128)S(1)}, f32[20]{0:T(128)}, u32[]{:S(2)}) copy-start(f32[20]{0:T(128)} %param.17) | copy-start | bytes 244
  0.7 1.0 %copy-start.8 = (s32[8]{0:T(128)S(1)}, s32[8]{0:T(128)}, u32[]{:S(2)}) copy-start(s32[8]{0:T(128)} %docs_ref.1) | copy-start | bytes 100
  1.8 1.1 %copy-start = (bf16[256,1280]{1,0:T(8,128)(2,1)S(1)}, bf16[256,1280]{1,0:T(8,128)(2,1)}, u32[]{:S(2)}) copy-start(bf16[256,1280]{1,0:T(8,128)(2,1)} %x_hbm.1) | copy-start | bytes 1966084
  2.8 1.1 %copy-start.1 = (bf16[256,1280]{1,0:T(8,128)(2,1)S(1)}, bf16[256,1280]{1,0:T(8,128)(2,1)}, u32[]{:S(2)}) copy-start(bf16[256,1280]{1,0:T(8,128)(2,1)} %gate_hbm.1) | copy-start | bytes 1966084

commit v3 on v2

--- a/solution.py
+++ b/solution.py
@@ -23,12 +23,13 @@
 
 def layer_kernel(
     groups, parts, heads,
-    x_hbm, gate_hbm, b_ref, c_ref, step_ref, bias_ref, rate_ref, taps_ref, shift_ref, gain_ref,
-    docs_ref, out_ref,
-    x, gate, steps, ext, halo, weighted, c_conv, rows_c, factor, ends, er, fr, wide,
-    carry_in, carry_out, qs, qr, q, dg, rs, sums, others,
-    x_sem, h_send, h_recv, f_send, f_recv, e_send, e_recv, z_send, z_recv, q_send, q_recv,
-    s_send, s_recv,
+    x_hbm, gate_hbm, b_hbm, c_hbm, step_hbm, bias_hbm, rate_hbm, taps_hbm, shift_hbm, gain_hbm,
+    docs_hbm, out_ref,
+    x, gate, b_ref, c_ref, step_ref, bias_ref, rate_ref, taps_ref, shift_ref, gain_ref, docs_ref,
+    turned, ext, halo, weighted, c_conv, rows_c, factor, ends, er, fr, wide,
+    z_factor, z_factors, z_total, z_totals, qs, qr, q, dg, rs, sums, others,
+    in_sem, h_send, h_recv, f_send, f_recv, e_send, e_recv, z_send, z_recv, zf_send, zf_recv,
+    q_send, q_recv, s_send, s_recv, ready,
 ):
     me, part = lax.axis_index("seq"), lax.axis_index("tp")
     shards = groups * SUPER
@@ -44,17 +45,15 @@
         to = ((dz + d // 16) % 2) * 16 + ((dy + (d // 4) % 4) % 4) * 4 + (dx + d % 4) % 4
         return to, group * SUPER + to
 
+    def hops(d):
+        along_y, along_x = (d // 4) % 4, d % 4
+        return d // 16 + min(along_y, 4 - along_y) + min(along_x, 4 - along_x)
+
+    farthest_first = sorted(range(1, SUPER), key=lambda d: (-hops(d), d % 4, d))
+
     def each(f):
-        def step(d, carry):
+        for d in farthest_first:
             f(d)
-            return carry
-
-        lax.fori_loop(1, SUPER, step, 0)
-
-    x_in = pltpu.make_async_copy(x_hbm, x, x_sem.at[0])
-    gate_in = pltpu.make_async_copy(gate_hbm, gate, x_sem.at[1])
-    x_in.start()
-    gate_in.start()
 
     barrier = pltpu.get_barrier_semaphore()
 
@@ -71,6 +70,24 @@
     pl.when(has_next & ends_group)(lambda: signal(seq=me + 1))
     pl.when(has_last & opens_group)(lambda: signal(seq=me - 1))
 
+    def fetch(k, source, target):
+        copy = pltpu.make_async_copy(source, target, in_sem.at[k])
+        copy.start()
+        return copy
+
+    step_in = fetch(0, step_hbm, step_ref)
+    bias_in = fetch(1, bias_hbm, bias_ref)
+    rate_in = fetch(2, rate_hbm, rate_ref)
+    docs_in = fetch(3, docs_hbm, docs_ref)
+    b_in = fetch(4, b_hbm, b_ref)
+    c_in = fetch(5, c_hbm, c_ref)
+    x_in = fetch(6, x_hbm, x)
+    taps_in = fetch(7, taps_hbm, taps_ref)
+    shift_in = fetch(8, shift_hbm, shift_ref)
+    gate_in = fetch(9, gate_hbm, gate)
+    gain_in = fetch(10, gain_hbm, gain_ref)
+
+    docs_in.wait()
     first = me * tokens
     starts, at = [], jnp.int32(0)
     for k in range(docs_ref.shape[0]):
@@ -88,29 +105,44 @@
     doc_row = locate(first + lax.broadcasted_iota(jnp.int32, (8, tokens), 1))
     doc_last = doc_row[0:1, tokens - 1 : tokens]
 
-    steps[...] = jnp.zeros_like(steps)
-    steps[:, :heads] = jax.nn.softplus(step_ref[...] + bias_ref[...])
-    rates = jnp.concatenate([rate_ref[...], jnp.zeros((1, 128 - heads), F32)], 1)
-    log_decay = -steps[...] * rates
+    step_in.wait()
+    bias_in.wait()
+    rate_in.wait()
+    same = lax.broadcasted_iota(jnp.int32, (heads, heads), 0) == lax.broadcasted_iota(
+        jnp.int32, (heads, heads), 1
+    )
+
+    def upright(row):
+        return jnp.sum(jnp.where(same, jnp.broadcast_to(row, (heads, heads)), 0.0), 1, keepdims=True)
+
+    step = jax.nn.softplus(step_ref[...] + upright(bias_ref[...]))
+    log_decay = -step * upright(rate_ref[...])
     order = lax.broadcasted_iota(jnp.int32, (tokens, tokens), 0)
     across = lax.broadcasted_iota(jnp.int32, (tokens, tokens), 1)
     lower = across <= order
     cumulated = jnp.dot(
-        lower.astype(F32), log_decay, precision=EXACT, preferred_element_type=F32
+        log_decay, (order <= across).astype(F32), precision=EXACT, preferred_element_type=F32
     )
     grown = jnp.exp(cumulated)
-    shrunk = jnp.exp(-cumulated) * steps[...]
-    last = grown[tokens - 1 : tokens, :]
-    rows_c[...] = shrunk.T
-    weights = jnp.where(doc == doc_last, shrunk * last, 0.0)
-    opened = jnp.where(doc < first, grown, 0.0)
-    factor[...] = opened[tokens - 1 : tokens, :]
+    shrunk = jnp.exp(-cumulated) * step
+    rows_c[...] = shrunk
+    turned[...] = jnp.zeros_like(turned)
+    turned[:heads, :] = grown
+    grown_c = turned[...].T
+    opened_c = jnp.where(doc < first, grown_c, 0.0)
+    factor[...] = opened_c[tokens - 1 : tokens, :]
+    turned[:heads, :] = jnp.where(
+        doc_row[0:1, :] == doc_last, shrunk * grown[:, tokens - 1 : tokens], 0.0
+    )
+    weights_c = turned[...].T
 
     count = (
         SUPER - 1 + parts - 1 + has_next.astype(jnp.int32) + has_last.astype(jnp.int32)
         + (has_next & ends_group).astype(jnp.int32) + (has_last & opens_group).astype(jnp.int32)
     )
     pl.semaphore_wait(barrier, count)
+    b_in.wait()
+    c_in.wait()
 
     def halo_copies():
         return [
@@ -153,8 +185,10 @@
     x_in.wait()
     for pair in range(pairs):
         cut = slice(128 * pair, 128 * pair + 128)
-        weighted[:, cut] = (x[:, cut].astype(F32) * spread(weights, pair)).astype(BF16)
-
+        weighted[:, cut] = (x[:, cut].astype(F32) * spread(weights_c, pair)).astype(BF16)
+
+    taps_in.wait()
+    shift_in.wait()
     ext[8:, :state] = b_ref[...].astype(F32)
     ext[8:, state:] = c_ref[...].astype(F32)
 
@@ -182,6 +216,23 @@
     b_turned = convolve(0).T.astype(BF16)
     ends[...] = jnp.dot(b_turned, weighted[...], preferred_element_type=F32)
     each(lambda d: e_copy(d).start())
+
+    for k in range(2, groups):
+        if k > 2:
+            @pl.when(group + k - 1 < groups)
+            def _():
+                pl.semaphore_wait(ready.at[k - 1], 1)
+
+        @pl.when(has_last & (group + k - 1 < groups))
+        def _():
+            pl.semaphore_signal(
+                ready.at[k], 1, device_id={"seq": me - SUPER}, device_id_type=MESH
+            )
+
+    @pl.when(group + groups - 1 < groups)
+    def _():
+        pl.semaphore_wait(ready.at[groups - 1], 1)
+
     fr[place] = factor[...]
     er[place] = ends[
         pl.ds(pl.multiple_of((place % 16) * rows, 8), rows),
@@ -199,7 +250,7 @@
         cut = slice(128 * pair, 128 * pair + 128)
         found = []
         for h in (2 * pair, 2 * pair + 1):
-            decay = jnp.broadcast_to(grown[:, h : h + 1], (tokens, 128))
+            decay = jnp.broadcast_to(grown_c[:, h : h + 1], (tokens, 128))
             row = rows_c[h : h + 1, :]
             low_scores = top * row[:, :half] * decay[:half]
             high = jnp.concatenate([decay[half:], decay[half:]], 1)
@@ -220,7 +271,7 @@
         opening = gate[:, cut].astype(F32)
         opening = opening * jax.nn.sigmoid(opening)
         dg[:, cut] = jnp.where(low, found[0], found[1]) * opening
-        rs[:, cut] = spread(opened, pair) * opening
+        rs[:, cut] = spread(opened_c, pair) * opening
 
     each(lambda d: f_copy(d).wait())
     column = lax.broadcasted_iota(jnp.int32, (128, lanes), 1) // width
@@ -228,33 +279,45 @@
     pick = (column == lax.broadcasted_iota(jnp.int32, (128, lanes), 0)).astype(F32)
     gathered = jnp.concatenate([fr[k] for k in range(SUPER)], 0)
     wide[...] = jnp.dot(gathered, pick, precision=EXACT, preferred_element_type=F32)
+
+    def zf_copy(k):
+        there = me + k * SUPER
+        return remote(z_factor, z_factors.at[group], zf_send.at[k], zf_recv.at[k], seq=there)
+
+    def z_copy(k):
+        there = me + k * SUPER
+        return remote(z_total, z_totals.at[group], z_send.at[k], z_recv.at[k], seq=there)
+
+    product = fr[0]
+    for k in range(1, SUPER):
+        product = product * fr[k]
+    z_factor[...] = product
+    for k in reversed(range(1, groups)):
+        pl.when(group + k < groups)(lambda: zf_copy(k).start())
     each(lambda d: e_copy(d).wait())
 
     def factor_of(k):
         return jnp.broadcast_to(wide[k : k + 1, :], (rows, lanes))
 
-    total, scale = er[0], factor_of(0)
+    total = er[0]
     for k in range(1, SUPER):
         total = factor_of(k) * total + er[k]
-        scale = factor_of(k) * scale
-
-    def z_copy():
-        return remote(carry_out, carry_in, z_send, z_recv, seq=me + SUPER)
-
-    @pl.when(has_last)
-    def _():
-        z_copy().wait_recv()
-
-    @pl.when(group == 0)
-    def _():
-        carry_in[...] = jnp.zeros_like(carry_in)
-
-    current = carry_in[...]
-    carry_out[...] = scale * current + total
-
-    @pl.when(has_next)
-    def _():
-        z_copy().start()
+    z_total[...] = total
+    for k in reversed(range(1, groups)):
+        pl.when(group + k < groups)(lambda: z_copy(k).start())
+    for k in range(1, groups):
+        @pl.when(group - k >= 0)
+        def _():
+            zf_copy(k).wait_recv()
+            z_copy(k).wait_recv()
+
+    passed = jnp.concatenate([z_factors[k] for k in range(groups)], 0)
+    passed = jnp.concatenate([passed] * (8 // groups), 0)
+    passed = jnp.dot(passed, pick, precision=EXACT, preferred_element_type=F32)
+    current = jnp.zeros((rows, lanes), F32)
+    for k in range(groups - 1):
+        scale = jnp.broadcast_to(passed[k : k + 1, :], (rows, lanes))
+        current = jnp.where(k < group, scale * current + z_totals[k], current)
 
     for k in range(SUPER):
         qs[k] = current.astype(BF16)
@@ -263,9 +326,11 @@
     each(lambda d: q_copy(d).start())
     qr[place] = qs[place]
 
-    @pl.when(has_next)
-    def _():
-        z_copy().wait_send()
+    for k in range(1, groups):
+        @pl.when(group + k < groups)
+        def _():
+            zf_copy(k).wait_send()
+            z_copy(k).wait_send()
 
     @pl.when(me + 1 < shards)
     def _():
@@ -299,9 +364,10 @@
     mean_square = (sums[...] + others[0] + others[1] + others[2]) * (1.0 / (features * parts))
     inverse = lax.rsqrt(mean_square + EPS)
     inverse = jnp.broadcast_to(inverse, (128, tokens)).T
+    gain_in.wait()
     for pair in range(pairs):
         cut = slice(128 * pair, 128 * pair + 128)
-        out_ref[:, cut] = (dg[:, cut] * inverse * gain_ref[:, cut]).astype(BF16)
+        out_ref[:, cut] = (dg[:, cut] * inverse * gain_ref[pair : pair + 1, :]).astype(BF16)
 
 
 def body(
@@ -314,29 +380,39 @@
     rows, lanes = state // 16, features // 2
     dma = pltpu.SemaphoreType.DMA
     vmem = pltpu.VMEM
-    whole = pl.BlockSpec(memory_space=pltpu.VMEM)
-    far = pl.BlockSpec(memory_space=pl.ANY)
+    far = pl.BlockSpec(memory_space=pltpu.HBM)
     return pl.pallas_call(
         functools.partial(layer_kernel, groups, parts, heads),
         out_shape=jax.ShapeDtypeStruct((tokens, features), BF16),
-        in_specs=[far, far] + [whole] * 8 + [pl.BlockSpec(memory_space=pltpu.SMEM)],
-        out_specs=whole,
+        in_specs=[far] * 11,
+        out_specs=pl.BlockSpec(memory_space=pltpu.VMEM),
         scratch_shapes=[
             vmem((tokens, features), BF16),
             vmem((tokens, features), BF16),
-            vmem((tokens, 128), F32),
+            vmem((tokens, state), BF16),
+            vmem((tokens, state), BF16),
+            vmem((heads, tokens), F32),
+            vmem((1, heads), F32),
+            vmem((1, heads), F32),
+            vmem(conv_weight.shape, F32),
+            vmem((1, 2 * state), F32),
+            vmem((features // 128, 128), F32),
+            pltpu.SMEM(doc_lengths.shape, jnp.int32),
+            vmem((128, tokens), F32),
             vmem((8 + tokens, 2 * state), F32),
             vmem((2, 16, state), BF16),
             vmem((tokens, features), BF16),
             vmem((tokens, state), BF16),
-            vmem((128, tokens), F32),
+            vmem((heads, tokens), F32),
             vmem((1, 128), F32),
             vmem((state, features), F32),
             vmem((SUPER, rows, lanes), F32),
             vmem((SUPER, 1, 128), F32),
             vmem((SUPER, lanes), F32),
+            vmem((1, 128), F32),
+            vmem((groups, 1, 128), F32),
             vmem((rows, lanes), F32),
-            vmem((rows, lanes), F32),
+            vmem((groups, rows, lanes), F32),
             vmem((SUPER, rows, lanes), BF16),
             vmem((SUPER, rows, lanes), BF16),
             vmem((state, features), BF16),
@@ -344,16 +420,18 @@
             vmem((tokens, features), F32),
             vmem((1, tokens), F32),
             vmem((parts - 1, 1, tokens), F32),
-            dma((2,)), dma((2,)), dma((2,)), dma((SUPER,)), dma((SUPER,)), dma((SUPER,)),
-            dma((SUPER,)), dma, dma, dma((SUPER,)), dma((SUPER,)),
-            dma((parts - 1,)), dma((parts - 1,)),
+            dma((11,)), dma((2,)), dma((2,)), dma((SUPER,)), dma((SUPER,)), dma((SUPER,)),
+            dma((SUPER,)), dma((groups,)), dma((groups,)), dma((groups,)), dma((groups,)),
+            dma((SUPER,)), dma((SUPER,)), dma((parts - 1,)), dma((parts - 1,)),
+            pltpu.SemaphoreType.REGULAR((groups,)),
         ],
         compiler_params=pltpu.CompilerParams(
-            collective_id=0, has_side_effects=True, vmem_limit_bytes=48 * 1024 * 1024
+            collective_id=0, has_side_effects=True, vmem_limit_bytes=67043328
         ),
     )(
-        inputs, gate_input, b_source, c_source, step_raw, step_bias[None, :],
-        decay_rate[None, :], conv_weight, conv_bias[None, :], norm_gain[None, :], doc_lengths,
+        inputs, gate_input, b_source, c_source, step_raw.T, step_bias[None, :],
+        decay_rate[None, :], conv_weight, conv_bias[None, :],
+        norm_gain.reshape(features // 128, 128), doc_lengths,
     )
 
 

time: 58.7 us -> 50.8 us (0.87)
  the two profiles are of different devices: /device:TPU:481 before, /device:TPU:65 now
where the time goes in v3:
time: 50.8 us; the launch traced here: 50.6 us
  Pallas kernels  48.6 us (96%)
  local copies, waits for them, and re-layouts  1.97 us (4%)
    pallas_call x1, Pallas kernels, body(): pl.pallas_call(functools.partial(layer_kernel, groups, parts, heads), out...  48.6 us
    unnamed x1, local copies, waits for them, and re-layouts  1.97 us

profile of v3, /device:TPU:65, one launch (start us, length us, event | category | flops | bytes accessed | tf_op | source)
XLA Modules:
  0.0 50.6 jit_solution(15160567716135829987)
XLA Ops:
  0.0 48.6 %shard_map.109 = bf16[256,1280]{1,0:T(8,128)(2,1)} custom-call(bf16[256,1280]{1,0:T(8,128)(2,1)} %x_hbm.1, bf16[256,1280]{1,0:T(8,128)(2,1)} %gate_hbm.1, bf16[256,128]{1,0:T(8,128)(2,1)} %b_hbm.1, bf16[256,128]{1,0:T(8,128)(2,1)} %c_hbm.1, f32[20,256]{1,0:T(8,128)} %bitcast.5, f32[1,20]{1,0:T(1,128)} %bitcast.8, f32[1,20]{1,0:T(1,128)} %bitcast.9, ...), custom_call_target="tpu_custom_call" | custom-call | tf_op jit(solution)/shard_map/pallas_call | solution.py:384
  48.6 2.0 %copy.13 = bf16[256,1280]{1,0:T(8,128)(2,1)} copy(bf16[256,1280]{1,0:T(8,128)(2,1)} %shard_map.109) | data formatting | bytes 1310720

commit v4 on v3

--- a/solution.py
+++ b/solution.py
@@ -75,17 +75,39 @@
         copy.start()
         return copy
 
+    b_in = fetch(4, b_hbm, b_ref)
+    c_in = fetch(5, c_hbm, c_ref)
     step_in = fetch(0, step_hbm, step_ref)
     bias_in = fetch(1, bias_hbm, bias_ref)
     rate_in = fetch(2, rate_hbm, rate_ref)
     docs_in = fetch(3, docs_hbm, docs_ref)
-    b_in = fetch(4, b_hbm, b_ref)
-    c_in = fetch(5, c_hbm, c_ref)
     x_in = fetch(6, x_hbm, x)
     taps_in = fetch(7, taps_hbm, taps_ref)
     shift_in = fetch(8, shift_hbm, shift_ref)
     gate_in = fetch(9, gate_hbm, gate)
     gain_in = fetch(10, gain_hbm, gain_ref)
+
+    count = (
+        SUPER - 1 + parts - 1 + has_next.astype(jnp.int32) + has_last.astype(jnp.int32)
+        + (has_next & ends_group).astype(jnp.int32) + (has_last & opens_group).astype(jnp.int32)
+    )
+    pl.semaphore_wait(barrier, count)
+    b_in.wait()
+    c_in.wait()
+
+    def halo_copies():
+        return [
+            remote(
+                ref.at[pl.ds(tokens - 16, 16), :], halo.at[k], h_send.at[k], h_recv.at[k],
+                seq=me + 1,
+            )
+            for k, ref in enumerate((b_ref, c_ref))
+        ]
+
+    @pl.when(me + 1 < shards)
+    def _():
+        for copy in halo_copies():
+            copy.start()
 
     docs_in.wait()
     first = me * tokens
@@ -136,30 +158,8 @@
     )
     weights_c = turned[...].T
 
-    count = (
-        SUPER - 1 + parts - 1 + has_next.astype(jnp.int32) + has_last.astype(jnp.int32)
-        + (has_next & ends_group).astype(jnp.int32) + (has_last & opens_group).astype(jnp.int32)
-    )
-    pl.semaphore_wait(barrier, count)
-    b_in.wait()
-    c_in.wait()
-
-    def halo_copies():
-        return [
-            remote(
-                ref.at[pl.ds(tokens - 16, 16), :], halo.at[k], h_send.at[k], h_recv.at[k],
-                seq=me + 1,
-            )
-            for k, ref in enumerate((b_ref, c_ref))
-        ]
-
-    @pl.when(me + 1 < shards)
-    def _():
-        for copy in halo_copies():
-            copy.start()
-
     def f_copy(d):
-        return remote(factor, fr.at[place], f_send.at[d], f_recv.at[d], seq=partner(d)[1])
+        return remote(factor, fr.at[place], f_send, f_recv, seq=partner(d)[1])
 
     def e_copy(d):
         to, there = partner(d)
@@ -167,11 +167,16 @@
             pl.ds(pl.multiple_of((to % 16) * rows, 8), rows),
             pl.ds(pl.multiple_of((to // 16) * lanes, 128), lanes),
         ]
-        return remote(source, er.at[place], e_send.at[d], e_recv.at[d], seq=there)
+        return remote(source, er.at[place], e_send, e_recv, seq=there)
 
     def q_copy(d):
         to, there = partner(d)
-        return remote(qs.at[to], qr.at[place], q_send.at[d], q_recv.at[d], seq=there)
+        return remote(qs.at[to], qr.at[place], q_send, q_recv, seq=there)
+
+    def wait_all(buffer, *sems):
+        part_of = buffer.at[pl.ds(0, SUPER - 1)]
+        for sem in sems:
+            pltpu.make_async_copy(part_of, part_of, sem).wait()
 
     each(lambda d: f_copy(d).start())
 
@@ -273,7 +278,7 @@
         dg[:, cut] = jnp.where(low, found[0], found[1]) * opening
         rs[:, cut] = spread(opened_c, pair) * opening
 
-    each(lambda d: f_copy(d).wait())
+    wait_all(fr, f_send, f_recv)
     column = lax.broadcasted_iota(jnp.int32, (128, lanes), 1) // width
     column = column + (place // 16) * (lanes // width)
     pick = (column == lax.broadcasted_iota(jnp.int32, (128, lanes), 0)).astype(F32)
@@ -294,7 +299,7 @@
     z_factor[...] = product
     for k in reversed(range(1, groups)):
         pl.when(group + k < groups)(lambda: zf_copy(k).start())
-    each(lambda d: e_copy(d).wait())
+    wait_all(er, e_send, e_recv)
 
     def factor_of(k):
         return jnp.broadcast_to(wide[k : k + 1, :], (rows, lanes))
@@ -337,7 +342,7 @@
         for copy in halo_copies():
             copy.wait_send()
 
-    each(lambda d: q_copy(d).wait())
+    wait_all(qr, q_send, q_recv)
     for side in range(2):
         for k in range(0, 16, 2):
             both = [qr[side * 16 + k + u].astype(F32) for u in range(2)]
@@ -381,6 +386,14 @@
     dma = pltpu.SemaphoreType.DMA
     vmem = pltpu.VMEM
     far = pl.BlockSpec(memory_space=pltpu.HBM)
+    pinned = [
+        pltpu.with_memory_space_constraint(a, pltpu.HBM)
+        for a in (
+            inputs, gate_input, b_source, c_source, step_raw.T, step_bias[None, :],
+            decay_rate[None, :], conv_weight, conv_bias[None, :],
+            norm_gain.reshape(features // 128, 128), doc_lengths,
+        )
+    ]
     return pl.pallas_call(
         functools.partial(layer_kernel, groups, parts, heads),
         out_shape=jax.ShapeDtypeStruct((tokens, features), BF16),
@@ -420,19 +433,15 @@
             vmem((tokens, features), F32),
             vmem((1, tokens), F32),
             vmem((parts - 1, 1, tokens), F32),
-            dma((11,)), dma((2,)), dma((2,)), dma((SUPER,)), dma((SUPER,)), dma((SUPER,)),
-            dma((SUPER,)), dma((groups,)), dma((groups,)), dma((groups,)), dma((groups,)),
-            dma((SUPER,)), dma((SUPER,)), dma((parts - 1,)), dma((parts - 1,)),
+            dma((11,)), dma((2,)), dma((2,)), dma, dma, dma, dma,
+            dma((groups,)), dma((groups,)), dma((groups,)), dma((groups,)),
+            dma, dma, dma((parts - 1,)), dma((parts - 1,)),
             pltpu.SemaphoreType.REGULAR((groups,)),
         ],
         compiler_params=pltpu.CompilerParams(
-            collective_id=0, has_side_effects=True, vmem_limit_bytes=67043328
+            collective_id=0, has_side_effects=True, vmem_limit_bytes=48 * 1024 * 1024
         ),
-    )(
-        inputs, gate_input, b_source, c_source, step_raw.T, step_bias[None, :],
-        decay_rate[None, :], conv_weight, conv_bias[None, :],
-        norm_gain.reshape(features // 128, 128), doc_lengths,
-    )
+    )(*pinned)
 
 
 def solution(mesh):

time: 50.8 us -> 47.1 us (0.927)
  Pallas kernels: 48.6 us -> 46.1 us
  local copies, waits for them, and re-layouts: 1.97 us -> 0.84 us
    pallas_call x1, Pallas kernels: 48.6 us -> 46.1 us  [body(): pl.pallas_call(functools.partial(layer_kernel, groups, parts, heads), out...]
    unnamed x1, local copies, waits for them, and re-layouts: 1.97 us -> 0.84 us
where the time goes in v4:
time: 47.1 us; the launch traced here: 47 us
  Pallas kernels  46.1 us (98%)
  local copies, waits for them, and re-layouts  0.84 us (2%)
    pallas_call x1, Pallas kernels, body(): pl.pallas_call(functools.partial(layer_kernel, groups, parts, heads), out...  46.1 us

profile of v4, /device:TPU:65, one launch (start us, length us, event | category | flops | bytes accessed | tf_op | source)
XLA Modules:
  0.0 47.0 jit_solution(11221191596153210880)
XLA Ops:
  0.0 46.1 %shard_map.109 = bf16[256,1280]{1,0:T(8,128)(2,1)S(1)} custom-call(bf16[256,1280]{1,0:T(8,128)(2,1)} %x_hbm.1, bf16[256,1280]{1,0:T(8,128)(2,1)} %gate_hbm.1, bf16[256,128]{1,0:T(8,128)(2,1)} %b_hbm.1, bf16[256,128]{1,0:T(8,128)(2,1)} %c_hbm.1, f32[20,256]{1,0:T(8,128)} %bitcast.5, f32[1,20]{1,0:T(1,128)} %bitcast.8, f32[1,20]{1,0:T(1,128)} %bitcast.9, ...), custom_call_target="tpu_custom_call" | custom-call | tf_op jit(solution)/shard_map/pallas_call | solution.py:397
  46.1 0.8 %copy.13 = bf16[256,1280]{1,0:T(8,128)(2,1)} copy(bf16[256,1280]{1,0:T(8,128)(2,1)S(1)} %shard_map.109) | data formatting | bytes 1310720

commit v5 on v4

--- a/solution.py
+++ b/solution.py
@@ -27,8 +27,8 @@
     docs_hbm, out_ref,
     x, gate, b_ref, c_ref, step_ref, bias_ref, rate_ref, taps_ref, shift_ref, gain_ref, docs_ref,
     turned, ext, halo, weighted, c_conv, rows_c, factor, ends, er, fr, wide,
-    z_factor, z_factors, z_total, z_totals, qs, qr, q, dg, rs, sums, others,
-    in_sem, h_send, h_recv, f_send, f_recv, e_send, e_recv, z_send, z_recv, zf_send, zf_recv,
+    z_factor, z_factor_in, z_total, z_total_in, z_state, z_state_in, qs, qr, q, dg, rs, sums, others,
+    in_sem, h_send, h_recv, f_send, f_recv, e_send, e_recv, z_send, z_recv,
     q_send, q_recv, s_send, s_recv, ready,
 ):
     me, part = lax.axis_index("seq"), lax.axis_index("tp")
@@ -60,15 +60,17 @@
     def signal(**device):
         pl.semaphore_signal(barrier, 1, device_id=device, device_id_type=MESH)
 
+    has_next, has_last = group + 1 < groups, group > 0
+    has_second = group + 2 < groups
+    ends_group, opens_group = place == SUPER - 1, place == 0
+    pl.when(has_last)(lambda: signal(seq=me - SUPER))
+    pl.when(has_last & opens_group)(lambda: signal(seq=me - 1))
     each(lambda d: signal(seq=partner(d)[1]))
-    for k in range(1, parts):
-        signal(tp=(part + k) % parts)
-    has_next, has_last = group + 1 < groups, group > 0
-    ends_group, opens_group = place == SUPER - 1, place == 0
     pl.when(has_next)(lambda: signal(seq=me + SUPER))
-    pl.when(has_last)(lambda: signal(seq=me - SUPER))
     pl.when(has_next & ends_group)(lambda: signal(seq=me + 1))
-    pl.when(has_last & opens_group)(lambda: signal(seq=me - 1))
+    chip_mate = part // 2 * 2 + 1 - part % 2
+    signal(tp=chip_mate)
+    upper = part // 2
 
     def fetch(k, source, target):
         copy = pltpu.make_async_copy(source, target, in_sem.at[k])
@@ -88,10 +90,16 @@
     gain_in = fetch(10, gain_hbm, gain_ref)
 
     count = (
-        SUPER - 1 + parts - 1 + has_next.astype(jnp.int32) + has_last.astype(jnp.int32)
+        SUPER - 1 + 1 + 2 * upper + has_next.astype(jnp.int32) + has_last.astype(jnp.int32)
         + (has_next & ends_group).astype(jnp.int32) + (has_last & opens_group).astype(jnp.int32)
     )
     pl.semaphore_wait(barrier, count)
+    for core in range(2):
+        signal(tp=(1 - upper) * 2 + core)
+    @pl.when(has_last & has_next)
+    def _():
+        pl.semaphore_signal(ready, 1, device_id={"seq": me - SUPER}, device_id_type=MESH)
+
     b_in.wait()
     c_in.wait()
 
@@ -221,22 +229,6 @@
     b_turned = convolve(0).T.astype(BF16)
     ends[...] = jnp.dot(b_turned, weighted[...], preferred_element_type=F32)
     each(lambda d: e_copy(d).start())
-
-    for k in range(2, groups):
-        if k > 2:
-            @pl.when(group + k - 1 < groups)
-            def _():
-                pl.semaphore_wait(ready.at[k - 1], 1)
-
-        @pl.when(has_last & (group + k - 1 < groups))
-        def _():
-            pl.semaphore_signal(
-                ready.at[k], 1, device_id={"seq": me - SUPER}, device_id_type=MESH
-            )
-
-    @pl.when(group + groups - 1 < groups)
-    def _():
-        pl.semaphore_wait(ready.at[groups - 1], 1)
 
     fr[place] = factor[...]
     er[place] = ends[
@@ -285,20 +277,28 @@
     gathered = jnp.concatenate([fr[k] for k in range(SUPER)], 0)
     wide[...] = jnp.dot(gathered, pick, precision=EXACT, preferred_element_type=F32)
 
-    def zf_copy(k):
-        there = me + k * SUPER
-        return remote(z_factor, z_factors.at[group], zf_send.at[k], zf_recv.at[k], seq=there)
-
-    def z_copy(k):
-        there = me + k * SUPER
-        return remote(z_total, z_totals.at[group], z_send.at[k], z_recv.at[k], seq=there)
-
     product = fr[0]
     for k in range(1, SUPER):
         product = product * fr[k]
     z_factor[...] = product
-    for k in reversed(range(1, groups)):
-        pl.when(group + k < groups)(lambda: zf_copy(k).start())
+
+    def factor_copy():
+        return remote(z_factor, z_factor_in, z_send.at[0], z_recv.at[0], seq=me + SUPER)
+
+    def total_copy():
+        return remote(z_total, z_total_in, z_send.at[1], z_recv.at[1], seq=me + SUPER)
+
+    def state_copy():
+        return remote(z_state, z_state_in, z_send.at[2], z_recv.at[2], seq=me + 2 * SUPER)
+
+    pl.when(has_next)(lambda: factor_copy().start())
+
+    def expand(row):
+        return jnp.dot(
+            jnp.broadcast_to(row, (rows, 128)), pick, precision=EXACT, preferred_element_type=F32
+        )
+
+    scale = expand(product)
     wait_all(er, e_send, e_recv)
 
     def factor_of(k):
@@ -308,21 +308,35 @@
     for k in range(1, SUPER):
         total = factor_of(k) * total + er[k]
     z_total[...] = total
-    for k in reversed(range(1, groups)):
-        pl.when(group + k < groups)(lambda: z_copy(k).start())
-    for k in range(1, groups):
-        @pl.when(group - k >= 0)
-        def _():
-            zf_copy(k).wait_recv()
-            z_copy(k).wait_recv()
-
-    passed = jnp.concatenate([z_factors[k] for k in range(groups)], 0)
-    passed = jnp.concatenate([passed] * (8 // groups), 0)
-    passed = jnp.dot(passed, pick, precision=EXACT, preferred_element_type=F32)
-    current = jnp.zeros((rows, lanes), F32)
-    for k in range(groups - 1):
-        scale = jnp.broadcast_to(passed[k : k + 1, :], (rows, lanes))
-        current = jnp.where(k < group, scale * current + z_totals[k], current)
+    pl.when(has_next)(lambda: total_copy().start())
+
+    @pl.when(group < 2)
+    def _():
+        z_state_in[...] = jnp.zeros_like(z_state_in)
+
+    @pl.when(group == 0)
+    def _():
+        z_factor_in[...] = jnp.zeros_like(z_factor_in)
+        z_total_in[...] = jnp.zeros_like(z_total_in)
+
+    @pl.when(has_last)
+    def _():
+        factor_copy().wait_recv()
+        total_copy().wait_recv()
+
+    scale_in = expand(z_factor_in[...])
+
+    @pl.when(group > 1)
+    def _():
+        state_copy().wait_recv()
+
+    current = scale_in * z_state_in[...] + z_total_in[...]
+    z_state[...] = scale * current + total
+
+    @pl.when(has_second)
+    def _():
+        pl.semaphore_wait(ready, 1)
+        state_copy().start()
 
     for k in range(SUPER):
         qs[k] = current.astype(BF16)
@@ -330,17 +344,6 @@
             current = factor_of(k) * current + er[k]
     each(lambda d: q_copy(d).start())
     qr[place] = qs[place]
-
-    for k in range(1, groups):
-        @pl.when(group + k < groups)
-        def _():
-            zf_copy(k).wait_send()
-            z_copy(k).wait_send()
-
-    @pl.when(me + 1 < shards)
-    def _():
-        for copy in halo_copies():
-            copy.wait_send()
 
     wait_all(qr, q_send, q_recv)
     for side in range(2):
@@ -362,8 +365,24 @@
         remote(sums, others.at[k - 1], s_send.at[k - 1], s_recv.at[k - 1], tp=(part + k) % parts)
         for k in range(1, parts)
     ]
+    @pl.when(upper == 0)
+    def _():
+        pl.semaphore_wait(barrier, 2)
+
     for copy in copies:
         copy.start()
+
+    @pl.when(me + 1 < shards)
+    def _():
+        for copy in halo_copies():
+            copy.wait_send()
+
+    @pl.when(has_next)
+    def _():
+        factor_copy().wait_send()
+        total_copy().wait_send()
+
+    pl.when(has_second)(lambda: state_copy().wait_send())
     for copy in copies:
         copy.wait()
     mean_square = (sums[...] + others[0] + others[1] + others[2]) * (1.0 / (features * parts))
@@ -423,9 +442,11 @@
             vmem((SUPER, 1, 128), F32),
             vmem((SUPER, lanes), F32),
             vmem((1, 128), F32),
-            vmem((groups, 1, 128), F32),
+            vmem((1, 128), F32),
             vmem((rows, lanes), F32),
-            vmem((groups, rows, lanes), F32),
+            vmem((rows, lanes), F32),
+            vmem((rows, lanes), F32),
+            vmem((rows, lanes), F32),
             vmem((SUPER, rows, lanes), BF16),
             vmem((SUPER, rows, lanes), BF16),
             vmem((state, features), BF16),
@@ -434,9 +455,9 @@
             vmem((1, tokens), F32),
             vmem((parts - 1, 1, tokens), F32),
             dma((11,)), dma((2,)), dma((2,)), dma, dma, dma, dma,
-            dma((groups,)), dma((groups,)), dma((groups,)), dma((groups,)),
+            dma((3,)), dma((3,)),
             dma, dma, dma((parts - 1,)), dma((parts - 1,)),
-            pltpu.SemaphoreType.REGULAR((groups,)),
+            pltpu.SemaphoreType.REGULAR,
         ],
         compiler_params=pltpu.CompilerParams(
             collective_id=0, has_side_effects=True, vmem_limit_bytes=48 * 1024 * 1024

time: 47.1 us -> 46.2 us (0.981)
  the two profiles are of different devices: /device:TPU:65 before, /device:TPU:1 now
where the time goes in v5:
time: 46.2 us; the launch traced here: 45.8 us
  Pallas kernels  44.9 us (97%)
  local copies, waits for them, and re-layouts  0.84 us (2%)
    pallas_call x1, Pallas kernels, body(): pl.pallas_call(functools.partial(layer_kernel, groups, parts, heads), out...  44.9 us

profile of v5, /device:TPU:1, one launch (start us, length us, event | category | flops | bytes accessed | tf_op | source)
XLA Modules:
  0.0 45.8 jit_solution(3323188661944290772)
XLA Ops:
  0.0 44.9 %shard_map.109 = bf16[256,1280]{1,0:T(8,128)(2,1)S(1)} custom-call(bf16[256,1280]{1,0:T(8,128)(2,1)} %x_hbm.1, bf16[256,1280]{1,0:T(8,128)(2,1)} %gate_hbm.1, bf16[256,128]{1,0:T(8,128)(2,1)} %b_hbm.1, bf16[256,128]{1,0:T(8,128)(2,1)} %c_hbm.1, f32[20,256]{1,0:T(8,128)} %bitcast.5, f32[1,20]{1,0:T(1,128)} %bitcast.8, f32[1,20]{1,0:T(1,128)} %bitcast.9, ...), custom_call_target="tpu_custom_call" | custom-call | tf_op jit(solution)/shard_map/pallas_call | solution.py:416
  44.9 0.8 %copy.13 = bf16[256,1280]{1,0:T(8,128)(2,1)} copy(bf16[256,1280]{1,0:T(8,128)(2,1)S(1)} %shard_map.109) | data formatting | bytes 1310720

commit v6 on v5

--- a/solution.py
+++ b/solution.py
@@ -10,6 +10,7 @@
 MESH = pl.DeviceIdType.MESH
 EPS = 1e-05
 SUPER = 32
+CODES = 32767.0
 F32 = jnp.float32
 BF16 = jnp.bfloat16
 EXACT = lax.Precision.HIGHEST
@@ -26,10 +27,11 @@
     x_hbm, gate_hbm, b_hbm, c_hbm, step_hbm, bias_hbm, rate_hbm, taps_hbm, shift_hbm, gain_hbm,
     docs_hbm, out_ref,
     x, gate, b_ref, c_ref, step_ref, bias_ref, rate_ref, taps_ref, shift_ref, gain_ref, docs_ref,
-    turned, ext, halo, weighted, c_conv, rows_c, factor, ends, er, fr, wide,
+    turned, ext, halo, weighted, c_conv, rows_c, factor, codes, grains, codes_in,
+    grains_in, er, fr, wide,
     z_factor, z_factor_in, z_total, z_total_in, z_state, z_state_in, qs, qr, q, dg, rs, sums, others,
-    in_sem, h_send, h_recv, f_send, f_recv, e_send, e_recv, z_send, z_recv,
-    q_send, q_recv, s_send, s_recv, ready,
+    in_sem, h_send, h_recv, f_send, f_recv, e_send, e_recv, g_send, g_recv, z_send, z_recv,
+    q_send, q_recv, s_send, s_recv, ready, here,
 ):
     me, part = lax.axis_index("seq"), lax.axis_index("tp")
     shards = groups * SUPER
@@ -72,6 +74,12 @@
     signal(tp=chip_mate)
     upper = part // 2
 
+    @pl.when(upper == 0)
+    def _():
+        for core in range(2):
+            signal(tp=2 + core)
+
+
     def fetch(k, source, target):
         copy = pltpu.make_async_copy(source, target, in_sem.at[k])
         copy.start()
@@ -94,8 +102,11 @@
         + (has_next & ends_group).astype(jnp.int32) + (has_last & opens_group).astype(jnp.int32)
     )
     pl.semaphore_wait(barrier, count)
-    for core in range(2):
-        signal(tp=(1 - upper) * 2 + core)
+    @pl.when(upper == 1)
+    def _():
+        for core in range(2):
+            pl.semaphore_signal(here, 1, device_id={"tp": core}, device_id_type=MESH)
+
     @pl.when(has_last & has_next)
     def _():
         pl.semaphore_signal(ready, 1, device_id={"seq": me - SUPER}, device_id_type=MESH)
@@ -171,11 +182,11 @@
 
     def e_copy(d):
         to, there = partner(d)
-        source = ends.at[
-            pl.ds(pl.multiple_of((to % 16) * rows, 8), rows),
-            pl.ds(pl.multiple_of((to // 16) * lanes, 128), lanes),
-        ]
-        return remote(source, er.at[place], e_send, e_recv, seq=there)
+        return remote(codes.at[to], codes_in.at[place], e_send, e_recv, seq=there)
+
+    def g_copy(d):
+        to, there = partner(d)
+        return remote(grains.at[to], grains_in.at[place], g_send, g_recv, seq=there)
 
     def q_copy(d):
         to, there = partner(d)
@@ -227,14 +238,25 @@
         return total * jax.nn.sigmoid(total)
 
     b_turned = convolve(0).T.astype(BF16)
-    ends[...] = jnp.dot(b_turned, weighted[...], preferred_element_type=F32)
-    each(lambda d: e_copy(d).start())
-
+    slices = SUPER // 2
+    for other in (1, 0):
+        side = (dz + other) % 2
+        ends = jnp.dot(
+            b_turned, weighted[:, pl.ds(pl.multiple_of(side * lanes, 128), lanes)],
+            preferred_element_type=F32,
+        ).reshape(slices, rows, lanes)
+        largest = jnp.maximum(jnp.max(jnp.abs(ends), 1, keepdims=True), 1e-30)
+        codes[pl.ds(side * slices, slices)] = (
+            jnp.round(ends * (CODES / largest)).astype(jnp.int32).astype(jnp.int16)
+        )
+        grains[pl.ds(side * slices, slices)] = largest * (1.0 / CODES)
+        for d in farthest_first:
+            if d // 16 == other:
+                e_copy(d).start()
+                g_copy(d).start()
     fr[place] = factor[...]
-    er[place] = ends[
-        pl.ds(pl.multiple_of((place % 16) * rows, 8), rows),
-        pl.ds(pl.multiple_of((place // 16) * lanes, 128), lanes),
-    ]
+    codes_in[place] = codes[place]
+    grains_in[place] = grains[place]
 
     c_conv[...] = convolve(1).astype(BF16)
     products = jnp.dot(c_conv[...], b_turned, preferred_element_type=F32)
@@ -299,7 +321,9 @@
         )
 
     scale = expand(product)
-    wait_all(er, e_send, e_recv)
+    wait_all(codes_in, e_send, e_recv)
+    wait_all(grains_in, g_send, g_recv)
+    er[...] = codes_in[...].astype(jnp.int32).astype(F32) * grains_in[...]
 
     def factor_of(k):
         return jnp.broadcast_to(wide[k : k + 1, :], (rows, lanes))
@@ -367,7 +391,7 @@
     ]
     @pl.when(upper == 0)
     def _():
-        pl.semaphore_wait(barrier, 2)
+        pl.semaphore_wait(here, 2)
 
     for copy in copies:
         copy.start()
@@ -437,7 +461,10 @@
             vmem((tokens, state), BF16),
             vmem((heads, tokens), F32),
             vmem((1, 128), F32),
-            vmem((state, features), F32),
+            vmem((SUPER, rows, lanes), jnp.int16),
+            vmem((SUPER, 1, lanes), F32),
+            vmem((SUPER, rows, lanes), jnp.int16),
+            vmem((SUPER, 1, lanes), F32),
             vmem((SUPER, rows, lanes), F32),
             vmem((SUPER, 1, 128), F32),
             vmem((SUPER, lanes), F32),
@@ -454,10 +481,10 @@
             vmem((tokens, features), F32),
             vmem((1, tokens), F32),
             vmem((parts - 1, 1, tokens), F32),
-            dma((11,)), dma((2,)), dma((2,)), dma, dma, dma, dma,
+            dma((11,)), dma((2,)), dma((2,)), dma, dma, dma, dma, dma, dma,
             dma((3,)), dma((3,)),
             dma, dma, dma((parts - 1,)), dma((parts - 1,)),
-            pltpu.SemaphoreType.REGULAR,
+            pltpu.SemaphoreType.REGULAR, pltpu.SemaphoreType.REGULAR,
         ],
         compiler_params=pltpu.CompilerParams(
             collective_id=0, has_side_effects=True, vmem_limit_bytes=48 * 1024 * 1024

time: 46.2 us -> 44.9 us (0.972)
  Pallas kernels: 44.9 us -> 43.2 us
    pallas_call x1, Pallas kernels: 44.9 us -> 43.2 us  [body(): pl.pallas_call(functools.partial(layer_kernel, groups, parts, heads), out...]
where the time goes in v6:
time: 44.9 us; the launch traced here: 44.1 us
  Pallas kernels  43.2 us (96%)
  local copies, waits for them, and re-layouts  0.84 us (2%)
    pallas_call x1, Pallas kernels, body(): pl.pallas_call(functools.partial(layer_kernel, groups, parts, heads), out...  43.2 us

profile of v6, /device:TPU:1, one launch (start us, length us, event | category | flops | bytes accessed | tf_op | source)
XLA Modules:
  0.0 44.1 jit_solution(6769657009153707820)
XLA Ops:
  0.0 43.2 %shard_map.109 = bf16[256,1280]{1,0:T(8,128)(2,1)S(1)} custom-call(bf16[256,1280]{1,0:T(8,128)(2,1)} %x_hbm.1, bf16[256,1280]{1,0:T(8,128)(2,1)} %gate_hbm.1, bf16[256,128]{1,0:T(8,128)(2,1)} %b_hbm.1, bf16[256,128]{1,0:T(8,128)(2,1)} %c_hbm.1, f32[20,256]{1,0:T(8,128)} %bitcast.5, f32[1,20]{1,0:T(1,128)} %bitcast.8, f32[1,20]{1,0:T(1,128)} %bitcast.9, ...), custom_call_target="tpu_custom_call" | custom-call | tf_op jit(solution)/shard_map/pallas_call | solution.py:440
  43.3 0.8 %copy.13 = bf16[256,1280]{1,0:T(8,128)(2,1)} copy(bf16[256,1280]{1,0:T(8,128)(2,1)S(1)} %shard_map.109) | data formatting | bytes 1310720
